TPU v7x, 256 devices: a whole 4x4x8 slice. The times are simulated.
256 devices in a mesh: seq: 64 (over z_lo, x, y), tp: 4 (over z_hi, core).
Axes of the slice: x: 4, y: 4, z: 8 (z_hi: 2, z_lo: 4; z = z_hi * 4 + z_lo), core: 2. Of those that a mesh axis runs over, the one named last changes fastest.
Arguments:
- states: bfloat16 [64, 128, 2048], P('seq', None, 'tp'), may hold values from -60 to 60, as said below
- cotangent: bfloat16 [64, 128, 2048], P('seq', None, 'tp'), may hold values from -12 to 12, as said below
- wq: bfloat16 [2048, 2048], P(None, 'tp'), may hold values from -0.125 to 0.125
- wk: bfloat16 [2048, 512], P(None, 'tp'), may hold values from -0.125 to 0.125
- wv: bfloat16 [2048, 512], P(None, 'tp'), may hold values from -0.125 to 0.125
- wo: bfloat16 [2048, 2048], P('tp'), may hold values from -0.125 to 0.125
Outputs:
- gram: float32 [64, 64], P('seq')
Inputs may be any that keep to these rules, and one draw needn't show every extreme that they name: `states`: finite values. `cotangent`: finite values.
All inputs are finite; a program needn't handle non-finite values.
Results may differ from a plain program's by a relative error of at most 0.0025.
Values may be sent and summed in bfloat16 or wider, within the bound.
No kernel may reach another device: no remote copies, remote signals or barrier semaphores. Data moves between devices by JAX's collectives and lax.ppermute only.
A program may use at most 64 MiB of HBM per device.

v0:
```python
import functools

import functools

import jax
import jax.numpy as jnp
import numpy as np
from jax import lax
from jax.experimental import pallas as pl
from jax.experimental.pallas import tpu as pltpu
from jax.sharding import Mesh
from jax.sharding import PartitionSpec as P


HEAD_DIM = 64
LANES = 128
SEQ = ("zb", "za", "x", "y")
NEAR = ("za", "x", "y")
TP = ("h", "c")
EVERY = SEQ + TP
SWAP = ((0, 1), (1, 0))


theta_base = 500000.0


def swapped(value, axis):
    return lax.ppermute(value, axis, SWAP)


def rope_tables(length, head_dim):
    half_dim = head_dim // 2
    steps = np.arange(half_dim, dtype=np.float32) * np.float32(2.0) / np.float32(head_dim)
    freqs_k = np.power(np.float32(theta_base), -steps)
    angles = np.arange(length, dtype=np.float32)[:, None] * freqs_k[None, :]
    sine = np.sin(angles)
    cos = np.tile(np.cos(angles), (1, LANES // half_dim))
    return cos, np.tile(np.concatenate([-sine, sine], axis=1), (1, LANES // head_dim))


def dot(left, right, dims=((1,), (0,))):
    return lax.dot_general(left, right, (dims, ((), ())), preferred_element_type=jnp.float32)


def kernel_call(body, outs, ins, scratch=(), vmem_mib=20, far=()):
    ins = [pltpu.with_memory_space_constraint(a, pltpu.HBM) if i in far else a for i, a in enumerate(ins)]
    hbm = pl.BlockSpec(memory_space=pltpu.HBM)
    smem = pl.BlockSpec(memory_space=pltpu.SMEM)
    vmem = pl.BlockSpec(memory_space=pltpu.VMEM)
    return pl.pallas_call(
        body,
        out_shape=outs,
        in_specs=[
            hbm if i in far else smem if a.dtype == jnp.int32 else vmem for i, a in enumerate(ins)
        ],
        out_specs=jax.tree.map(lambda _: vmem, outs),
        scratch_shapes=scratch,
        compiler_params=pltpu.CompilerParams(vmem_limit_bytes=vmem_mib * 2**20),
    )(*ins)


def lower_half(shape):
    return lax.broadcasted_iota(jnp.int32, shape, 1) % (2 * HEAD_DIM) < HEAD_DIM


def doubled(pair, low):
    turned = pltpu.roll(pair, HEAD_DIM, 1)
    return jnp.where(low, pair, turned), jnp.where(low, turned, pair)


def rows_at(place, size):
    return pl.ds(pl.multiple_of(place * size, size), size)


def places_of(at):
    h, c = at[0], at[1]
    return [2 * h + c, 2 * h + 1 - c, 2 * (1 - h) + c, 2 * (1 - h) + 1 - c]


def own_quarters(parts):
    values = [part[...] for part in parts]
    far = [jnp.concatenate([values[2 + k], values[4 + k]], axis=0) for k in range(2)]
    return values[:2] + far


def partner_quarters(at, parts):
    straight = at[2] == 0
    values = [part[...] for part in parts]
    up, down = values[:2], values[2:]
    here = [jnp.where(straight, d, u) for u, d in zip(up, down)]
    return here + [jnp.where(straight, u, d) for u, d in zip(up, down)]


def fetch_body(at, wq, wk, wv, wo, wq_out, wk_out, wv_out, wo_out, sems):
    part = wq_out.shape[1]
    half = rows_at(at[2], part)
    moves = [
        pltpu.make_async_copy(src, dst, sems.at[i])
        for i, (src, dst) in enumerate(
            ((wq.at[:, half], wq_out), (wk, wk_out), (wv, wv_out), (wo.at[half, :], wo_out))
        )
    ]
    for move in moves:
        move.start()
    for move in moves:
        move.wait()


def attention_body(partner, at, *refs):
    *found, wq, wk, wv, cos_ref, sine_ref, attended, probs = refs
    parts = partner_quarters(at, found) if partner else own_quarters(found)
    quarter = parts[0].shape[1]

    def project(w):
        total = None
        for part, place in zip(parts, places_of(at)):
            term = dot(part, w[rows_at(place, quarter), :])
            total = term if total is None else total + term
        return total

    cos, sine = cos_ref[...], sine_ref[...]
    length = cos.shape[0]
    lane = lax.broadcasted_iota(jnp.int32, cos.shape, 1)
    first = lane % HEAD_DIM < HEAD_DIM // 2
    low = lower_half(cos.shape)
    straight = at[2] == 0

    def rotate(tile):
        ahead = pltpu.roll(tile, LANES - HEAD_DIM // 2, 1)
        behind = pltpu.roll(tile, HEAD_DIM // 2, 1)
        return tile * cos + jnp.where(first, ahead, behind) * sine

    def own_head(tile):
        even, odd = doubled(tile, low)
        return jnp.where(straight, even, odd).astype(jnp.bfloat16)

    keys, values, queries = own_head(rotate(project(wk))), own_head(project(wv)), project(wq)
    causal = lax.broadcasted_iota(jnp.int32, (length, length), 0) >= lax.broadcasted_iota(
        jnp.int32, (length, length), 1
    )
    for t in range(queries.shape[1] // LANES):
        query = rotate(queries[:, t * LANES : (t + 1) * LANES])
        found = []
        for s in range(2):
            mine = low if s == 0 else jnp.logical_not(low)
            q = jnp.where(mine, query, 0.0).astype(jnp.bfloat16)
            scores = dot(q, keys, ((1,), (1,))) * HEAD_DIM ** (-0.5)
            scores = jnp.where(causal, scores, -jnp.inf)
            e = jnp.exp(scores - jnp.max(scores, axis=1, keepdims=True))
            p = (e / jnp.sum(e, axis=1, keepdims=True)).astype(jnp.bfloat16)
            probs[(2 * t + s) * length : (2 * t + s + 1) * length, :] = p
            found.append(dot(p, values))
        tile = jnp.where(low, found[0], found[1])
        attended[:, t * LANES : (t + 1) * LANES] = tile.astype(jnp.bfloat16)


def blocks_body(at, *refs):
    s_refs, c_refs = refs[:10], refs[10:20]
    wo, attended_own, probs_own, attended_partner, probs_partner, blocks = refs[20:]
    attended, probs = (attended_own, attended_partner), (probs_own, probs_partner)
    states = list(zip(own_quarters(s_refs[:6]), partner_quarters(at, s_refs[6:])))
    cots = list(zip(own_quarters(c_refs[:6]), partner_quarters(at, c_refs[6:])))
    places = places_of(at)
    length, quarter = states[0][0].shape
    grads = None
    for pair, place in zip(cots, places):
        term = dot(jnp.concatenate(pair, axis=0), wo[:, rows_at(place, quarter)], ((1,), (1,)))
        grads = term if grads is None else grads + term
    low = lower_half((length, LANES))
    width = attended_own.shape[1]
    tiles = width // LANES
    tall = blocks.shape[1] // 2
    across = 4 * quarter // LANES
    for n in range(2):
        rows = slice(n * length, (n + 1) * length)
        stacked = []
        for t in range(tiles):
            tile = grads[rows, t * LANES : (t + 1) * LANES]
            stacked.append(jnp.where(low, tile, 0.0).astype(jnp.bfloat16))
            stacked.append(jnp.where(low, 0.0, tile).astype(jnp.bfloat16))
        found = dot(probs[n][...], jnp.concatenate(stacked, 0), ((0,), (0,)))
        value_gradient = (found + pltpu.roll(found, HEAD_DIM, 1)).astype(jnp.bfloat16)
        turned_a = attended[n][...].T
        turned_v = value_gradient.T[:HEAD_DIM, :]
        for k, place in enumerate(places):
            upper = dot(turned_a, cots[k][n]).astype(jnp.bfloat16)
            lower = dot(turned_v, states[k][n]).astype(jnp.bfloat16)
            for j in range(quarter // LANES):
                cols = slice(j * LANES, (j + 1) * LANES)
                at_col = place * (quarter // LANES) + j
                begin = n * tall
                blocks[at_col, begin : begin + tall, :] = upper[:tall, cols]
                rest = width - tall
                blocks[across + at_col, begin : begin + rest, :] = upper[tall:, cols]
                blocks[across + at_col, begin + rest : begin + tall, :] = lower[:, cols]


def share_body(at, got, rows_out, wide):
    seqs, both, _ = got.shape
    tall = both // 2
    straight = at[2] == 0
    for s in range(seqs):
        wide[pl.ds(s * both, both), :] = got[s].astype(jnp.float32)

    def rows_of(r):
        found = [
            wide[pl.ds(r + k * tall, seqs, stride=both), :].astype(jnp.bfloat16) for k in range(2)
        ]
        return jnp.concatenate(
            [jnp.where(straight, found[0], found[1]), jnp.where(straight, found[1], found[0])], axis=0
        )

    total = jnp.zeros((2 * seqs, 2 * seqs), jnp.float32)
    for r in range(0, tall, 2):
        x = jnp.concatenate([rows_of(r), rows_of(r + 1)], axis=1)
        total = total + dot(x, x, ((1,), (1,)))
    eye = lax.broadcasted_iota(jnp.int32, total.shape, 0) == lax.broadcasted_iota(
        jnp.int32, total.shape, 1
    )
    diag = jnp.sum(jnp.where(eye, total, 0.0), axis=0, keepdims=True)
    rows = jnp.concatenate([total, jnp.broadcast_to(diag, total.shape)], axis=1)
    copies = rows_out.shape[0] // rows.shape[0]
    for k in range(copies):
        rows_out[pl.ds(k, rows.shape[0], stride=copies), :] = rows


def final_body(at, got, out):
    seqs = out.shape[1]
    total = jnp.sum(got[...], axis=0, keepdims=True)
    lane = lax.broadcasted_iota(jnp.int32, total.shape, 1)
    own_diag = jnp.sum(jnp.where(lane == at[3] + seqs, total, 0.0), axis=1, keepdims=True)
    diag = pltpu.roll(total, seqs, 1)
    out[...] = (total / jnp.sqrt(own_diag * diag))[:, :seqs]


def on_device(states, cotangent, wq, wk, wv, wo):
    bf16, f32 = jnp.bfloat16, jnp.float32
    shape = jax.ShapeDtypeStruct
    length, part = states.shape[1:]
    states, cotangent = states[0], cotangent[0]
    axes = (lax.axis_index("h"), lax.axis_index("c"), lax.axis_index("zb"), lax.axis_index(SEQ))
    at = jnp.stack(axes).astype(jnp.int32)
    blocks = lax.axis_size(NEAR)
    seqs = 2 * blocks
    tall = (part + LANES) * (2 * part) // (LANES * blocks)

    def around(step):
        ring = (0, 2, 1, 3)
        return [(ring[q], ring[(q + step) % 4]) for q in range(4)]

    def moved(piece, step):
        return lax.ppermute(piece, ("zb", "h"), around(step))

    def near(piece):
        return piece, swapped(piece, "c")

    def gathered(own):
        up, down = moved(own, 1), moved(own, -1)
        half = length // 2
        low, high = moved(up[:half], 1), moved(down[half:], -1)
        kinds = (own, low, high, up, down)
        return [part for piece in kinds for part in near(piece)]

    s_parts, c_parts = gathered(states), gathered(cotangent)
    cos, sine = rope_tables(length, HEAD_DIM)
    width = part // 2
    wq, wk, wv, wo = kernel_call(
        fetch_body,
        tuple(
            shape(dims, bf16)
            for dims in ((wq.shape[0], width), wk.shape, wv.shape, (width, wo.shape[1]))
        ),
        (at, wq, wk, wv, wo),
        (pltpu.SemaphoreType.DMA((4,)),),
        far=(1, 2, 3, 4),
    )

    def attention(partner, parts):
        return kernel_call(
            functools.partial(attention_body, partner),
            (
                shape((length, width), bf16),
                shape((width // HEAD_DIM * length, length), bf16),
            ),
            (at, *parts, wq, wk, wv, cos, sine),
        )

    partner_found = attention(True, s_parts[6:])
    own_found = attention(False, s_parts[:6])
    sent = kernel_call(
        blocks_body,
        shape((blocks, 2 * tall, LANES), bf16),
        (at, *s_parts, *c_parts, wo, *own_found, *partner_found),
    )
    got = lax.all_to_all(sent, NEAR, 0, 0, tiled=True)
    copies = lax.axis_size(TP)
    rows = kernel_call(
        share_body,
        shape((seqs * copies, 2 * seqs), f32),
        (at, got),
        (pltpu.VMEM((seqs * tall, LANES), f32),),
    )
    rows = rows.reshape(seqs * copies, 1, 2 * seqs)
    got = lax.all_to_all(rows, EVERY, 0, 0, tiled=True).reshape(seqs * copies, 2 * seqs)
    return kernel_call(final_body, shape((1, seqs), f32), (at, got))


def solution(mesh):
    split = Mesh(mesh.devices.reshape(2, mesh.shape["seq"] // 32, 4, 4, 2, 2), EVERY)
    placed = (
        P(SEQ, None, TP),
        P(SEQ, None, TP),
        P(None, TP),
        P(None, TP),
        P(None, TP),
        P(TP, None),
    )

    return jax.shard_map(
        on_device, mesh=split, in_specs=placed, out_specs=P(SEQ, None), check_vma=False
    )
```

profile of v0, /device:TPU:1, one launch (start us, length us, event | category | flops | bytes accessed | tf_op | source)
XLA Modules:
  0.0 110.2 jit_solution(10478755647893388201)
XLA Ops:
  0.0 6.8 %collective-permute-start.4 = (bf16[128,512]{1,0:T(8,128)(2,1)}, bf16[128,512]{1,0:T(8,128)(2,1)S(1)}, u32[]{:S(2)}, u32[]{:S(2)}) collective-permute-start(bf16[128,512]{1,0:T(8,128)(2,1)} %bitcast.10), channel_id=1, source_target_pairs={{0,130},{128,0},{2,128},{130,2},{1,131},{129,1},{3,129},{131,3},{4... | collective-permute-start | bytes 393224 | tf_op jit(solution)/shard_map/ppermute | solution.py:252
  6.8 3.6 %collective-permute-start.13 = (bf16[128,512]{1,0:T(8,128)(2,1)}, bf16[128,512]{1,0:T(8,128)(2,1)S(1)}, u32[]{:S(2)}, u32[]{:S(2)}) collective-permute-start(bf16[128,512]{1,0:T(8,128)(2,1)} %bitcast.17), channel_id=1, source_target_pairs={{0,130},{128,0},{2,128},{130,2},{1,131},{129,1},{3,129},{131,3},{4... | collective-permute-start | bytes 393224 | tf_op jit(solution)/shard_map/ppermute | solution.py:252
  10.4 1.5 %collective-permute-start = (bf16[128,512]{1,0:T(8,128)(2,1)}, bf16[128,512]{1,0:T(8,128)(2,1)S(1)}, u32[]{:S(2)}, u32[]{:S(2)}) collective-permute-start(bf16[128,512]{1,0:T(8,128)(2,1)} %bitcast.12), channel_id=1, source_target_pairs={{0,1},{1,0},{2,3},{3,2},{4,5},{5,4},{6,7},{7,6},{8,9},{9,8},{10,11... | collective-permute-start | bytes 393224 | tf_op jit(solution)/shard_map/ppermute | solution.py:28
  11.9 3.6 %collective-permute-start.5 = (bf16[64,512]{1,0:T(8,128)(2,1)S(1)}, bf16[64,512]{1,0:T(8,128)(2,1)S(1)}, u32[]{:S(2)}, u32[]{:S(2)}) collective-permute-start(bf16[64,512]{1,0:T(8,128)(2,1)S(1)} %slice.17), channel_id=1, source_target_pairs={{0,130},{128,0},{2,128},{130,2},{1,131},{129,1},{3,129},{131,3},{4... | collective-permute-start | bytes 196616 | tf_op jit(solution)/shard_map/ppermute | solution.py:252
  15.7 0.2 collective-permute-done.13.refs_18_
  15.9 2.7 %collective-permute-start.8 = (bf16[128,512]{1,0:T(8,128)(2,1)S(1)}, bf16[128,512]{1,0:T(8,128)(2,1)S(1)}, u32[]{:S(2)}, u32[]{:S(2)}) collective-permute-start(bf16[128,512]{1,0:T(8,128)(2,1)S(1)} %collective-permute-done.4.refs_2_.refs_8_), channel_id=1, source_target_pairs={{0,1},{1,0},{2,3},{3,2},{4,5},{5,4},{6,7},{7,6},{8,9},{9,8},{10,11... | collective-permute-start | bytes 393224 | tf_op jit(solution)/shard_map/ppermute | solution.py:28
  18.6 4.4 %collective-permute-start.14 = (bf16[64,512]{1,0:T(8,128)(2,1)S(1)}, bf16[64,512]{1,0:T(8,128)(2,1)S(1)}, u32[]{:S(2)}, u32[]{:S(2)}) collective-permute-start(bf16[64,512]{1,0:T(8,128)(2,1)S(1)} %slice.19), channel_id=1, source_target_pairs={{0,130},{128,0},{2,128},{130,2},{1,131},{129,1},{3,129},{131,3},{4... | collective-permute-start | bytes 196616 | tf_op jit(solution)/shard_map/ppermute | solution.py:252
  23.0 0.5 collective-permute-done.10.refs_16_
  23.6 0.5 collective-permute-start.7
  24.1 0.9 collective-permute-done.2.refs_2_
  25.1 0.4 collective-permute-start.6
  25.5 0.1 collective-permute-start.3
  25.6 4.2 %collective-permute-done.11.refs_12_ = bf16[64,512]{1,0:T(8,128)(2,1)S(1)} collective-permute-done((bf16[64,512]{1,0:T(8,128)(2,1)S(1)}, bf16[64,512]{1,0:T(8,128)(2,1)S(1)}, u32[]{:S(2)}, u32[]{:S(2)}) %collective-permute-start.11) | collective-permute-done | bytes 65568 | tf_op jit(solution)/shard_map/ppermute | solution.py:252
  29.8 1.6 %collective-permute-start.9 = (bf16[128,512]{1,0:T(8,128)(2,1)}, bf16[128,512]{1,0:T(8,128)(2,1)S(1)}, u32[]{:S(2)}, u32[]{:S(2)}) collective-permute-start(bf16[128,512]{1,0:T(8,128)(2,1)} %bitcast.19), channel_id=1, source_target_pairs={{0,1},{1,0},{2,3},{3,2},{4,5},{5,4},{6,7},{7,6},{8,9},{9,8},{10,11... | collective-permute-start | bytes 393224 | tf_op jit(solution)/shard_map/ppermute | solution.py:28
  31.5 0.5 collective-permute-start.16
  32.1 0.4 collective-permute-start.12
  32.6 2.4 %shard_map.82 = (bf16[2048,256]{1,0:T(8,128)(2,1)S(1)}, bf16[2048,128]{1,0:T(8,128)(2,1)S(1)}, bf16[2048,128]{1,0:T(8,128)(2,1)S(1)}, bf16[256,2048]{1,0:T(8,128)(2,1)S(1)}) custom-call(s32[4]{0:T(128)S(1)} %pad_add_fusion.at, bf16[2048,512]{1,0:T(8,128)(2,1)} %wq.1, bf16[2048,128]{1,0:T(8,128)(2,1)} %wk.1, bf16[2048,128]{1,0:T(8,128)(2,1)} %wv.1, ...), custom_call_target="tpu_custom_call" | custom-call | tf_op jit(solution)/shard_map/pallas_call | solution.py:50
  35.1 2.7 %shard_map.84 = (bf16[128,256]{1,0:T(8,128)(2,1)S(1)}, bf16[512,128]{1,0:T(8,128)(2,1)S(1)}) custom-call(s32[4]{0:T(128)S(1)} %pad_add_fusion.at, bf16[128,512]{1,0:T(8,128)(2,1)S(1)} %collective-permute-done.1.refs_0_.refs_6_, bf16[128,512]{1,0:T(8,128)(2,1)S(1)} %collective-permute-done.7.refs_1_.refs_7_, ...), custom_call_target="tpu_custom_call" | custom-call | tf_op jit(solution)/shard_map/pallas_call | solution.py:50
  37.7 2.7 %shard_map.83 = (bf16[128,256]{1,0:T(8,128)(2,1)S(1)}, bf16[512,128]{1,0:T(8,128)(2,1)S(1)}) custom-call(s32[4]{0:T(128)S(1)} %pad_add_fusion.at, bf16[128,512]{1,0:T(8,128)(2,1)S(1)} %bitcast.13, bf16[128,512]{1,0:T(8,128)(2,1)S(1)} %collective-permute-done.refs_1_, bf16[64,512]{1,0:T(8,128)(2,1)S(1)} %collective-permute-done.2.refs_2_, ...), custom_call_target="tpu_custom_call" | custom-call | tf_op jit(solution)/shard_map/pallas_call | solution.py:50
  40.5 2.7 %shard_map.85 = bf16[32,320,128]{2,1,0:T(8,128)(2,1)S(1)} custom-call(s32[4]{0:T(128)S(1)} %pad_add_fusion.at, bf16[128,512]{1,0:T(8,128)(2,1)S(1)} %bitcast.14, bf16[128,512]{1,0:T(8,128)(2,1)S(1)} %collective-permute-done.refs_1_, bf16[64,512]{1,0:T(8,128)(2,1)S(1)} %collective-permute-done.2.refs_2_, bf16[64,512]{1,0:T(8,128)(2,1)S(1)} %collective-permute-done.3.refs_3_, ...), custom_call_target="tpu_custom_call" | custom-call | tf_op jit(solution)/shard_map/pallas_call | solution.py:50
  43.2 41.0 %all_to_all.10.got = bf16[32,320,128]{2,1,0:T(8,128)(2,1)S(1)} all-to-all(bf16[32,320,128]{2,1,0:T(8,128)(2,1)S(1)} %shard_map.85), channel_id=1, replica_groups=mesh['zb'=2,'za'=2,'x'=4,'y'=4,'h'=2,'c'=2] {'za','x','y'}, dimensions={0} | all-to-all | bytes 5242880 | tf_op jit(solution)/shard_map/all_to_all | solution.py:295
  84.2 4.5 %shard_map.86 = f32[256,128]{1,0:T(8,128)S(1)} custom-call(s32[4]{0:T(128)S(1)} %pad_add_fusion.at, bf16[32,320,128]{2,1,0:T(8,128)(2,1)S(1)} %all_to_all.10.got), custom_call_target="tpu_custom_call" | custom-call | tf_op jit(solution)/shard_map/pallas_call | solution.py:50
  88.7 20.3 %all_to_all.11 = f32[256,1,128]{2,1,0:T(1,128)S(1)} all-to-all(f32[256,1,128]{2,1,0:T(1,128)S(1)} %bitcast.15), channel_id=1, replica_groups=mesh['zb'=2,'za'=2,'x'=4,'y'=4,'h'=2,'c'=2] {'zb','za','x','y','h','c'}, dimensions={0} | all-to-all | bytes 262144 | tf_op jit(solution)/shard_map/all_to_all | solution.py:304
  109.0 1.2 %shard_map.87 = f32[1,64]{1,0:T(1,128)} custom-call(s32[4]{0:T(128)S(1)} %pad_add_fusion.at, f32[256,128]{1,0:T(8,128)S(1)} %bitcast.16), custom_call_target="tpu_custom_call" | custom-call | tf_op jit(solution)/shard_map/pallas_call | solution.py:50
  (33 shorter events, 0.4 us)
Async XLA Ops:
  0.0 11.9 %collective-permute-start.4 = (bf16[128,512]{1,0:T(8,128)(2,1)}, bf16[128,512]{1,0:T(8,128)(2,1)S(1)}, u32[]{:S(2)}, u32[]{:S(2)}) collective-permute-start(bf16[128,512]{1,0:T(8,128)(2,1)} %bitcast.10), channel_id=1, source_target_pairs={{0,130},{128,0},{2,128},{130,2},{1,131},{129,1},{3,129},{131,3},{4... | collective-permute-start | bytes 393224 | tf_op jit(solution)/shard_map/ppermute | solution.py:252
  6.8 8.8 %collective-permute-start.1 = (bf16[128,512]{1,0:T(8,128)(2,1)}, bf16[128,512]{1,0:T(8,128)(2,1)S(1)}, u32[]{:S(2)}, u32[]{:S(2)}) collective-permute-start(bf16[128,512]{1,0:T(8,128)(2,1)} %bitcast.11), channel_id=1, source_target_pairs={{0,128},{128,2},{2,130},{130,0},{1,129},{129,3},{3,131},{131,1},{4... | collective-permute-start | bytes 393224 | tf_op jit(solution)/shard_map/ppermute | solution.py:252
  6.8 9.1 %collective-permute-start.13 = (bf16[128,512]{1,0:T(8,128)(2,1)}, bf16[128,512]{1,0:T(8,128)(2,1)S(1)}, u32[]{:S(2)}, u32[]{:S(2)}) collective-permute-start(bf16[128,512]{1,0:T(8,128)(2,1)} %bitcast.17), channel_id=1, source_target_pairs={{0,130},{128,0},{2,128},{130,2},{1,131},{129,1},{3,129},{131,3},{4... | collective-permute-start | bytes 393224 | tf_op jit(solution)/shard_map/ppermute | solution.py:252
  10.4 8.2 %collective-permute-start = (bf16[128,512]{1,0:T(8,128)(2,1)}, bf16[128,512]{1,0:T(8,128)(2,1)S(1)}, u32[]{:S(2)}, u32[]{:S(2)}) collective-permute-start(bf16[128,512]{1,0:T(8,128)(2,1)} %bitcast.12), channel_id=1, source_target_pairs={{0,1},{1,0},{2,3},{3,2},{4,5},{5,4},{6,7},{7,6},{8,9},{9,8},{10,11... | collective-permute-start | bytes 393224 | tf_op jit(solution)/shard_map/ppermute | solution.py:28
  11.9 11.7 %collective-permute-start.10 = (bf16[128,512]{1,0:T(8,128)(2,1)}, bf16[128,512]{1,0:T(8,128)(2,1)S(1)}, u32[]{:S(2)}, u32[]{:S(2)}) collective-permute-start(bf16[128,512]{1,0:T(8,128)(2,1)} %bitcast.18), channel_id=1, source_target_pairs={{0,128},{128,2},{2,130},{130,0},{1,129},{129,3},{3,131},{131,1},{4... | collective-permute-start | bytes 393224 | tf_op jit(solution)/shard_map/ppermute | solution.py:252
  11.9 12.1 %collective-permute-start.5 = (bf16[64,512]{1,0:T(8,128)(2,1)S(1)}, bf16[64,512]{1,0:T(8,128)(2,1)S(1)}, u32[]{:S(2)}, u32[]{:S(2)}) collective-permute-start(bf16[64,512]{1,0:T(8,128)(2,1)S(1)} %slice.17), channel_id=1, source_target_pairs={{0,130},{128,0},{2,128},{130,2},{1,131},{129,1},{3,129},{131,3},{4... | collective-permute-start | bytes 196616 | tf_op jit(solution)/shard_map/ppermute | solution.py:252
  15.6 9.5 %collective-permute-start.2 = (bf16[64,512]{1,0:T(8,128)(2,1)S(1)}, bf16[64,512]{1,0:T(8,128)(2,1)S(1)}, u32[]{:S(2)}, u32[]{:S(2)}) collective-permute-start(bf16[64,512]{1,0:T(8,128)(2,1)S(1)} %slice.16), channel_id=1, source_target_pairs={{0,128},{128,2},{2,130},{130,0},{1,129},{129,3},{3,131},{131,1},{4... | collective-permute-start | bytes 196616 | tf_op jit(solution)/shard_map/ppermute | solution.py:252
  15.9 15.5 %collective-permute-start.8 = (bf16[128,512]{1,0:T(8,128)(2,1)S(1)}, bf16[128,512]{1,0:T(8,128)(2,1)S(1)}, u32[]{:S(2)}, u32[]{:S(2)}) collective-permute-start(bf16[128,512]{1,0:T(8,128)(2,1)S(1)} %collective-permute-done.4.refs_2_.refs_8_), channel_id=1, source_target_pairs={{0,1},{1,0},{2,3},{3,2},{4,5},{5,4},{6,7},{7,6},{8,9},{9,8},{10,11... | collective-permute-start | bytes 393224 | tf_op jit(solution)/shard_map/ppermute | solution.py:28
  18.6 6.9 %collective-permute-start.14 = (bf16[64,512]{1,0:T(8,128)(2,1)S(1)}, bf16[64,512]{1,0:T(8,128)(2,1)S(1)}, u32[]{:S(2)}, u32[]{:S(2)}) collective-permute-start(bf16[64,512]{1,0:T(8,128)(2,1)S(1)} %slice.19), channel_id=1, source_target_pairs={{0,130},{128,0},{2,128},{130,2},{1,131},{129,1},{3,129},{131,3},{4... | collective-permute-start | bytes 196616 | tf_op jit(solution)/shard_map/ppermute | solution.py:252
  23.6 8.5 %collective-permute-start.7 = (bf16[128,512]{1,0:T(8,128)(2,1)S(1)}, bf16[128,512]{1,0:T(8,128)(2,1)S(1)}, u32[]{:S(2)}, u32[]{:S(2)}) collective-permute-start(bf16[128,512]{1,0:T(8,128)(2,1)S(1)} %collective-permute-done.1.refs_0_.refs_6_), channel_id=1, source_target_pairs={{0,1},{1,0},{2,3},{3,2},{4,5},{5,4},{6,7},{7,6},{8,9},{9,8},{10,11... | collective-permute-start | bytes 393224 | tf_op jit(solution)/shard_map/ppermute | solution.py:28
  24.0 5.8 %collective-permute-start.11 = (bf16[64,512]{1,0:T(8,128)(2,1)S(1)}, bf16[64,512]{1,0:T(8,128)(2,1)S(1)}, u32[]{:S(2)}, u32[]{:S(2)}) collective-permute-start(bf16[64,512]{1,0:T(8,128)(2,1)S(1)} %slice.18), channel_id=1, source_target_pairs={{0,128},{128,2},{2,130},{130,0},{1,129},{129,3},{3,131},{131,1},{4... | collective-permute-start | bytes 196616 | tf_op jit(solution)/shard_map/ppermute | solution.py:252
  25.1 6.4 %collective-permute-start.6 = (bf16[64,512]{1,0:T(8,128)(2,1)S(1)}, bf16[64,512]{1,0:T(8,128)(2,1)S(1)}, u32[]{:S(2)}, u32[]{:S(2)}) collective-permute-start(bf16[64,512]{1,0:T(8,128)(2,1)S(1)} %collective-permute-done.5.refs_4_), channel_id=1, source_target_pairs={{0,1},{1,0},{2,3},{3,2},{4,5},{5,4},{6,7},{7,6},{8,9},{9,8},{10,11... | collective-permute-start | bytes 196616 | tf_op jit(solution)/shard_map/ppermute | solution.py:28
  25.5 6.5 %collective-permute-start.3 = (bf16[64,512]{1,0:T(8,128)(2,1)S(1)}, bf16[64,512]{1,0:T(8,128)(2,1)S(1)}, u32[]{:S(2)}, u32[]{:S(2)}) collective-permute-start(bf16[64,512]{1,0:T(8,128)(2,1)S(1)} %collective-permute-done.2.refs_2_), channel_id=1, source_target_pairs={{0,1},{1,0},{2,3},{3,2},{4,5},{5,4},{6,7},{7,6},{8,9},{9,8},{10,11... | collective-permute-start | bytes 196616 | tf_op jit(solution)/shard_map/ppermute | solution.py:28
  29.8 10.6 %collective-permute-start.9 = (bf16[128,512]{1,0:T(8,128)(2,1)}, bf16[128,512]{1,0:T(8,128)(2,1)S(1)}, u32[]{:S(2)}, u32[]{:S(2)}) collective-permute-start(bf16[128,512]{1,0:T(8,128)(2,1)} %bitcast.19), channel_id=1, source_target_pairs={{0,1},{1,0},{2,3},{3,2},{4,5},{5,4},{6,7},{7,6},{8,9},{9,8},{10,11... | collective-permute-start | bytes 393224 | tf_op jit(solution)/shard_map/ppermute | solution.py:28
  31.4 9.0 %collective-permute-start.17 = (bf16[128,512]{1,0:T(8,128)(2,1)S(1)}, bf16[128,512]{1,0:T(8,128)(2,1)S(1)}, u32[]{:S(2)}, u32[]{:S(2)}) collective-permute-start(bf16[128,512]{1,0:T(8,128)(2,1)S(1)} %collective-permute-done.13.refs_18_), channel_id=1, source_target_pairs={{0,1},{1,0},{2,3},{3,2},{4,5},{5,4},{6,7},{7,6},{8,9},{9,8},{10,11... | collective-permute-start | bytes 393224 | tf_op jit(solution)/shard_map/ppermute | solution.py:28
  31.5 9.0 %collective-permute-start.16 = (bf16[128,512]{1,0:T(8,128)(2,1)S(1)}, bf16[128,512]{1,0:T(8,128)(2,1)S(1)}, u32[]{:S(2)}, u32[]{:S(2)}) collective-permute-start(bf16[128,512]{1,0:T(8,128)(2,1)S(1)} %collective-permute-done.10.refs_16_), channel_id=1, source_target_pairs={{0,1},{1,0},{2,3},{3,2},{4,5},{5,4},{6,7},{7,6},{8,9},{9,8},{10,11... | collective-permute-start | bytes 393224 | tf_op jit(solution)/shard_map/ppermute | solution.py:28
  32.0 8.5 %collective-permute-start.15 = (bf16[64,512]{1,0:T(8,128)(2,1)S(1)}, bf16[64,512]{1,0:T(8,128)(2,1)S(1)}, u32[]{:S(2)}, u32[]{:S(2)}) collective-permute-start(bf16[64,512]{1,0:T(8,128)(2,1)S(1)} %collective-permute-done.14.refs_14_), channel_id=1, source_target_pairs={{0,1},{1,0},{2,3},{3,2},{4,5},{5,4},{6,7},{7,6},{8,9},{9,8},{10,11... | collective-permute-start | bytes 196616 | tf_op jit(solution)/shard_map/ppermute | solution.py:28
  32.1 8.4 %collective-permute-start.12 = (bf16[64,512]{1,0:T(8,128)(2,1)S(1)}, bf16[64,512]{1,0:T(8,128)(2,1)S(1)}, u32[]{:S(2)}, u32[]{:S(2)}) collective-permute-start(bf16[64,512]{1,0:T(8,128)(2,1)S(1)} %collective-permute-done.11.refs_12_), channel_id=1, source_target_pairs={{0,1},{1,0},{2,3},{3,2},{4,5},{5,4},{6,7},{7,6},{8,9},{9,8},{10,11... | collective-permute-start | bytes 196616 | tf_op jit(solution)/shard_map/ppermute | solution.py:28
  32.6 2.5 %copy-start.1 = (f32[128,128]{1,0:T(8,128)S(1)}, f32[128,128]{1,0:T(8,128)}, u32[]{:S(2)}) copy-start(f32[128,128]{1,0:T(8,128)} %constant.34.clone.refs_10_.refs_8_) | copy-start | bytes 196612
  32.6 2.5 %copy-start.2 = (f32[128,128]{1,0:T(8,128)S(1)}, f32[128,128]{1,0:T(8,128)}, u32[]{:S(2)}) copy-start(f32[128,128]{1,0:T(8,128)} %constant.33.clone.refs_9_.refs_7_) | copy-start | bytes 196612
  35.0 2.7 %copy-start = (bf16[1,128,512]{2,1,0:T(8,128)(2,1)S(1)}, bf16[1,128,512]{2,1,0:T(8,128)(2,1)}, u32[]{:S(2)}) copy-start(bf16[1,128,512]{2,1,0:T(8,128)(2,1)} %param.8) | copy-start | bytes 393220
  35.0 5.4 %copy-start.3 = (bf16[1,128,512]{2,1,0:T(8,128)(2,1)S(1)}, bf16[1,128,512]{2,1,0:T(8,128)(2,1)}, u32[]{:S(2)}) copy-start(bf16[1,128,512]{2,1,0:T(8,128)(2,1)} %param.9) | copy-start | bytes 393220
where the time goes:
time: 110 us
  blocking collectives  61.3 us (56%)
  starting transfers between devices  26.4 us (24%)
  Pallas kernels  16.1 us (15%)
  waiting for transfers between devices  5.99 us (5%)
    all_to_all x1, blocking collectives, on_device(): got = lax.all_to_all(sent, NEAR, 0, 0, tiled=True)  41 us
    all_to_all x1, blocking collectives, on_device(): lax.all_to_all(rows, EVERY, 0, 0, tiled=True)  20.3 us
    ppermute x8, starting transfers between devices, moved(): return lax.ppermute(piece, ('zb', 'h'), around(step))  18.7 us
    pallas_call x6, Pallas kernels, kernel_call(): pl.pallas_call(body, out_shape=outs, in_specs=[hbm if i in far else smem...  16.1 us
    ppermute x10, starting transfers between devices, swapped(): return lax.ppermute(value, axis, SWAP)  7.77 us
    ppermute x8, waiting for transfers between devices, moved(): return lax.ppermute(piece, ('zb', 'h'), around(step))  5.96 us
  transfers between devices with their start and end apart: 18, of which 4 were waited for; matrix products, arithmetic and copies ran while one was open for 0% of the time, Pallas kernels for 7%

commit v1 on v0

--- a/solution.py
+++ b/solution.py
@@ -78,9 +78,7 @@
 
 
 def own_quarters(parts):
-    values = [part[...] for part in parts]
-    far = [jnp.concatenate([values[2 + k], values[4 + k]], axis=0) for k in range(2)]
-    return values[:2] + far
+    return [part[...] for part in parts]
 
 
 def partner_quarters(at, parts):
@@ -155,11 +153,11 @@
 
 
 def blocks_body(at, *refs):
-    s_refs, c_refs = refs[:10], refs[10:20]
-    wo, attended_own, probs_own, attended_partner, probs_partner, blocks = refs[20:]
+    s_refs, c_refs = refs[:8], refs[8:16]
+    wo, attended_own, probs_own, attended_partner, probs_partner, blocks = refs[16:]
     attended, probs = (attended_own, attended_partner), (probs_own, probs_partner)
-    states = list(zip(own_quarters(s_refs[:6]), partner_quarters(at, s_refs[6:])))
-    cots = list(zip(own_quarters(c_refs[:6]), partner_quarters(at, c_refs[6:])))
+    states = list(zip(own_quarters(s_refs[:4]), partner_quarters(at, s_refs[4:])))
+    cots = list(zip(own_quarters(c_refs[:4]), partner_quarters(at, c_refs[4:])))
     places = places_of(at)
     length, quarter = states[0][0].shape
     grads = None
@@ -254,14 +252,13 @@
     def near(piece):
         return piece, swapped(piece, "c")
 
-    def gathered(own):
+    def gathered(own, relayed):
         up, down = moved(own, 1), moved(own, -1)
-        half = length // 2
-        low, high = moved(up[:half], 1), moved(down[half:], -1)
-        kinds = (own, low, high, up, down)
+        far = moved(up if relayed == 1 else down, relayed)
+        kinds = (own, far, up, down)
         return [part for piece in kinds for part in near(piece)]
 
-    s_parts, c_parts = gathered(states), gathered(cotangent)
+    s_parts, c_parts = gathered(states, 1), gathered(cotangent, -1)
     cos, sine = rope_tables(length, HEAD_DIM)
     width = part // 2
     wq, wk, wv, wo = kernel_call(
@@ -285,8 +282,8 @@
             (at, *parts, wq, wk, wv, cos, sine),
         )
 
-    partner_found = attention(True, s_parts[6:])
-    own_found = attention(False, s_parts[:6])
+    partner_found = attention(True, s_parts[4:])
+    own_found = attention(False, s_parts[:4])
     sent = kernel_call(
         blocks_body,
         shape((blocks, 2 * tall, LANES), bf16),

time: 110 us -> 108 us (0.982)
  starting transfers between devices: 26.4 us -> 23.7 us
    ppermute x8 -> x6, starting transfers between devices: 18.7 us -> 16.5 us  [moved(): return lax.ppermute(piece, ('zb', 'h'), around(step))]
    all_to_all x1, blocking collectives: 20.3 us -> 22.2 us  [on_device(): lax.all_to_all(rows, EVERY, 0, 0, tiled=True)]
    all_to_all x1, blocking collectives: 41 us -> 39.7 us  [on_device(): got = lax.all_to_all(sent, NEAR, 0, 0, tiled=True)]
    ppermute x10 -> x8, starting transfers between devices: 7.77 us -> 7.21 us  [swapped(): return lax.ppermute(value, axis, SWAP)]
    ppermute x8 -> x6, waiting for transfers between devices: 5.96 us -> 6.2 us  [moved(): return lax.ppermute(piece, ('zb', 'h'), around(step))]
  transfers between devices with their start and end apart: 18 -> 14, of which waited for: 4 -> 5; matrix products, arithmetic and copies ran while one was open for 0% -> 0% of each run, Pallas kernels for 7% -> 7%
where the time goes in v1:
time: 108 us
  blocking collectives  61.9 us (57%)
  starting transfers between devices  23.7 us (22%)
  Pallas kernels  16.1 us (15%)
  waiting for transfers between devices  6.22 us (6%)
    all_to_all x1, blocking collectives, on_device(): got = lax.all_to_all(sent, NEAR, 0, 0, tiled=True)  39.7 us
    all_to_all x1, blocking collectives, on_device(): lax.all_to_all(rows, EVERY, 0, 0, tiled=True)  22.2 us
    ppermute x6, starting transfers between devices, moved(): return lax.ppermute(piece, ('zb', 'h'), around(step))  16.5 us
    pallas_call x6, Pallas kernels, kernel_call(): pl.pallas_call(body, out_shape=outs, in_specs=[hbm if i in far else smem...  16.1 us
    ppermute x8, starting transfers between devices, swapped(): return lax.ppermute(value, axis, SWAP)  7.21 us
    ppermute x6, waiting for transfers between devices, moved(): return lax.ppermute(piece, ('zb', 'h'), around(step))  6.2 us
  transfers between devices with their start and end apart: 14, of which 5 were waited for; matrix products, arithmetic and copies ran while one was open for 0% of the time, Pallas kernels for 7%

profile of v1, /device:TPU:1, one launch (start us, length us, event | category | flops | bytes accessed | tf_op | source)
XLA Modules:
  0.0 108.2 jit_solution(17530745161141053611)
XLA Ops:
  0.0 3.8 %collective-permute-start.1 = (bf16[128,512]{1,0:T(8,128)(2,1)}, bf16[128,512]{1,0:T(8,128)(2,1)S(1)}, u32[]{:S(2)}, u32[]{:S(2)}) collective-permute-start(bf16[128,512]{1,0:T(8,128)(2,1)} %bitcast.10), channel_id=1, source_target_pairs={{0,128},{128,2},{2,130},{130,0},{1,129},{129,3},{3,131},{131,1},{4... | collective-permute-start | bytes 393224 | tf_op jit(solution)/shard_map/ppermute | solution.py:250
  3.8 3.0 %collective-permute-start.5 = (bf16[128,512]{1,0:T(8,128)(2,1)}, bf16[128,512]{1,0:T(8,128)(2,1)S(1)}, u32[]{:S(2)}, u32[]{:S(2)}) collective-permute-start(bf16[128,512]{1,0:T(8,128)(2,1)} %bitcast.11), channel_id=1, source_target_pairs={{0,130},{128,0},{2,128},{130,2},{1,131},{129,1},{3,129},{131,3},{4... | collective-permute-start | bytes 393224 | tf_op jit(solution)/shard_map/ppermute | solution.py:250
  6.8 1.0 collective-permute-start
  7.8 2.6 %collective-permute-start.8 = (bf16[128,512]{1,0:T(8,128)(2,1)}, bf16[128,512]{1,0:T(8,128)(2,1)S(1)}, u32[]{:S(2)}, u32[]{:S(2)}) collective-permute-start(bf16[128,512]{1,0:T(8,128)(2,1)} %bitcast.17), channel_id=1, source_target_pairs={{0,130},{128,0},{2,128},{130,2},{1,131},{129,1},{3,129},{131,3},{4... | collective-permute-start | bytes 393224 | tf_op jit(solution)/shard_map/ppermute | solution.py:250
  10.4 0.4 collective-permute-done.1.refs_0_.refs_4_
  10.8 4.6 %collective-permute-start.2 = (bf16[128,512]{1,0:T(8,128)(2,1)S(1)}, bf16[128,512]{1,0:T(8,128)(2,1)S(1)}, u32[]{:S(2)}, u32[]{:S(2)}) collective-permute-start(bf16[128,512]{1,0:T(8,128)(2,1)S(1)} %collective-permute-done.1.refs_0_.refs_4_), channel_id=1, source_target_pairs={{0,128},{128,2},{2,130},{130,0},{1,129},{129,3},{3,131},{131,1},{4... | collective-permute-start | bytes 393224 | tf_op jit(solution)/shard_map/ppermute | solution.py:250
  15.5 1.9 %collective-permute-done.5.refs_2_.refs_6_ = bf16[128,512]{1,0:T(8,128)(2,1)S(1)} collective-permute-done((bf16[128,512]{1,0:T(8,128)(2,1)}, bf16[128,512]{1,0:T(8,128)(2,1)S(1)}, u32[]{:S(2)}, u32[]{:S(2)}) %collective-permute-start.5) | collective-permute-done | bytes 131104 | tf_op jit(solution)/shard_map/ppermute | solution.py:250
  17.4 1.5 %collective-permute-start.6 = (bf16[128,512]{1,0:T(8,128)(2,1)S(1)}, bf16[128,512]{1,0:T(8,128)(2,1)S(1)}, u32[]{:S(2)}, u32[]{:S(2)}) collective-permute-start(bf16[128,512]{1,0:T(8,128)(2,1)S(1)} %collective-permute-done.5.refs_2_.refs_6_), channel_id=1, source_target_pairs={{0,1},{1,0},{2,3},{3,2},{4,5},{5,4},{6,7},{7,6},{8,9},{9,8},{10,11... | collective-permute-start | bytes 393224 | tf_op jit(solution)/shard_map/ppermute | solution.py:28
  18.9 1.3 %collective-permute-done.8.refs_14_ = bf16[128,512]{1,0:T(8,128)(2,1)S(1)} collective-permute-done((bf16[128,512]{1,0:T(8,128)(2,1)}, bf16[128,512]{1,0:T(8,128)(2,1)S(1)}, u32[]{:S(2)}, u32[]{:S(2)}) %collective-permute-start.8) | collective-permute-done | bytes 131104 | tf_op jit(solution)/shard_map/ppermute | solution.py:250
  20.2 2.4 %collective-permute-start.9 = (bf16[128,512]{1,0:T(8,128)(2,1)S(1)}, bf16[128,512]{1,0:T(8,128)(2,1)S(1)}, u32[]{:S(2)}, u32[]{:S(2)}) collective-permute-start(bf16[128,512]{1,0:T(8,128)(2,1)S(1)} %collective-permute-done.8.refs_14_), channel_id=1, source_target_pairs={{0,130},{128,0},{2,128},{130,2},{1,131},{129,1},{3,129},{131,3},{4... | collective-permute-start | bytes 393224 | tf_op jit(solution)/shard_map/ppermute | solution.py:250
  22.5 1.3 %collective-permute-start.7 = (bf16[128,512]{1,0:T(8,128)(2,1)}, bf16[128,512]{1,0:T(8,128)(2,1)S(1)}, u32[]{:S(2)}, u32[]{:S(2)}) collective-permute-start(bf16[128,512]{1,0:T(8,128)(2,1)} %bitcast.19), channel_id=1, source_target_pairs={{0,1},{1,0},{2,3},{3,2},{4,5},{5,4},{6,7},{7,6},{8,9},{9,8},{10,11... | collective-permute-start | bytes 393224 | tf_op jit(solution)/shard_map/ppermute | solution.py:28
  23.8 1.1 collective-permute-done.2.refs_2_
  24.9 1.8 %collective-permute-start.3 = (bf16[128,512]{1,0:T(8,128)(2,1)S(1)}, bf16[128,512]{1,0:T(8,128)(2,1)S(1)}, u32[]{:S(2)}, u32[]{:S(2)}) collective-permute-start(bf16[128,512]{1,0:T(8,128)(2,1)S(1)} %collective-permute-done.2.refs_2_), channel_id=1, source_target_pairs={{0,1},{1,0},{2,3},{3,2},{4,5},{5,4},{6,7},{7,6},{8,9},{9,8},{10,11... | collective-permute-start | bytes 393224 | tf_op jit(solution)/shard_map/ppermute | solution.py:28
  26.7 0.5 collective-permute-start.12
  27.2 1.5 %collective-permute-done.9.refs_10_ = bf16[128,512]{1,0:T(8,128)(2,1)S(1)} collective-permute-done((bf16[128,512]{1,0:T(8,128)(2,1)S(1)}, bf16[128,512]{1,0:T(8,128)(2,1)S(1)}, u32[]{:S(2)}, u32[]{:S(2)}) %collective-permute-start.9) | collective-permute-done | bytes 131104 | tf_op jit(solution)/shard_map/ppermute | solution.py:250
  28.7 1.2 %collective-permute-start.10 = (bf16[128,512]{1,0:T(8,128)(2,1)S(1)}, bf16[128,512]{1,0:T(8,128)(2,1)S(1)}, u32[]{:S(2)}, u32[]{:S(2)}) collective-permute-start(bf16[128,512]{1,0:T(8,128)(2,1)S(1)} %collective-permute-done.9.refs_10_), channel_id=1, source_target_pairs={{0,1},{1,0},{2,3},{3,2},{4,5},{5,4},{6,7},{7,6},{8,9},{9,8},{10,11... | collective-permute-start | bytes 393224 | tf_op jit(solution)/shard_map/ppermute | solution.py:28
  30.0 2.4 %shard_map.82 = (bf16[2048,256]{1,0:T(8,128)(2,1)S(1)}, bf16[2048,128]{1,0:T(8,128)(2,1)S(1)}, bf16[2048,128]{1,0:T(8,128)(2,1)S(1)}, bf16[256,2048]{1,0:T(8,128)(2,1)S(1)}) custom-call(s32[4]{0:T(128)S(1)} %pad_add_fusion.at, bf16[2048,512]{1,0:T(8,128)(2,1)} %wq.1, bf16[2048,128]{1,0:T(8,128)(2,1)} %wk.1, bf16[2048,128]{1,0:T(8,128)(2,1)} %wv.1, ...), custom_call_target="tpu_custom_call" | custom-call | tf_op jit(solution)/shard_map/pallas_call | solution.py:50
  32.5 2.7 %shard_map.84 = (bf16[128,256]{1,0:T(8,128)(2,1)S(1)}, bf16[512,128]{1,0:T(8,128)(2,1)S(1)}) custom-call(s32[4]{0:T(128)S(1)} %pad_add_fusion.at, bf16[128,512]{1,0:T(8,128)(2,1)S(1)} %collective-permute-done.1.refs_0_.refs_4_, bf16[128,512]{1,0:T(8,128)(2,1)S(1)} %collective-permute-done.4.refs_1_.refs_5_, ...), custom_call_target="tpu_custom_call" | custom-call | tf_op jit(solution)/shard_map/pallas_call | solution.py:50
  35.2 2.7 %shard_map.83 = (bf16[128,256]{1,0:T(8,128)(2,1)S(1)}, bf16[512,128]{1,0:T(8,128)(2,1)S(1)}) custom-call(s32[4]{0:T(128)S(1)} %pad_add_fusion.at, bf16[128,512]{1,0:T(8,128)(2,1)S(1)} %bitcast.13, bf16[128,512]{1,0:T(8,128)(2,1)S(1)} %collective-permute-done.refs_1_, bf16[128,512]{1,0:T(8,128)(2,1)S(1)} %collective-permute-done.2.refs_2_, ...), custom_call_target="tpu_custom_call" | custom-call | tf_op jit(solution)/shard_map/pallas_call | solution.py:50
  37.9 2.7 %shard_map.85 = bf16[32,320,128]{2,1,0:T(8,128)(2,1)S(1)} custom-call(s32[4]{0:T(128)S(1)} %pad_add_fusion.at, bf16[128,512]{1,0:T(8,128)(2,1)S(1)} %bitcast.14, bf16[128,512]{1,0:T(8,128)(2,1)S(1)} %collective-permute-done.refs_1_, bf16[128,512]{1,0:T(8,128)(2,1)S(1)} %collective-permute-done.2.refs_2_, ...), custom_call_target="tpu_custom_call" | custom-call | tf_op jit(solution)/shard_map/pallas_call | solution.py:50
  40.6 39.7 %all_to_all.10.got = bf16[32,320,128]{2,1,0:T(8,128)(2,1)S(1)} all-to-all(bf16[32,320,128]{2,1,0:T(8,128)(2,1)S(1)} %shard_map.85), channel_id=1, replica_groups=mesh['zb'=2,'za'=2,'x'=4,'y'=4,'h'=2,'c'=2] {'za','x','y'}, dimensions={0} | all-to-all | bytes 5242880 | tf_op jit(solution)/shard_map/all_to_all | solution.py:292
  80.4 4.5 %shard_map.86 = f32[256,128]{1,0:T(8,128)S(1)} custom-call(s32[4]{0:T(128)S(1)} %pad_add_fusion.at, bf16[32,320,128]{2,1,0:T(8,128)(2,1)S(1)} %all_to_all.10.got), custom_call_target="tpu_custom_call" | custom-call | tf_op jit(solution)/shard_map/pallas_call | solution.py:50
  84.8 22.2 %all_to_all.11 = f32[256,1,128]{2,1,0:T(1,128)S(1)} all-to-all(f32[256,1,128]{2,1,0:T(1,128)S(1)} %bitcast.15), channel_id=1, replica_groups=mesh['zb'=2,'za'=2,'x'=4,'y'=4,'h'=2,'c'=2] {'zb','za','x','y','h','c'}, dimensions={0} | all-to-all | bytes 262144 | tf_op jit(solution)/shard_map/all_to_all | solution.py:301
  107.0 1.2 %shard_map.87 = f32[1,64]{1,0:T(1,128)} custom-call(s32[4]{0:T(128)S(1)} %pad_add_fusion.at, f32[256,128]{1,0:T(8,128)S(1)} %bitcast.16), custom_call_target="tpu_custom_call" | custom-call | tf_op jit(solution)/shard_map/pallas_call | solution.py:50
  (21 shorter events, 0.1 us)
Async XLA Ops:
  0.0 10.8 %collective-permute-start.1 = (bf16[128,512]{1,0:T(8,128)(2,1)}, bf16[128,512]{1,0:T(8,128)(2,1)S(1)}, u32[]{:S(2)}, u32[]{:S(2)}) collective-permute-start(bf16[128,512]{1,0:T(8,128)(2,1)} %bitcast.10), channel_id=1, source_target_pairs={{0,128},{128,2},{2,130},{130,0},{1,129},{129,3},{3,131},{131,1},{4... | collective-permute-start | bytes 393224 | tf_op jit(solution)/shard_map/ppermute | solution.py:250
  3.8 13.6 %collective-permute-start.5 = (bf16[128,512]{1,0:T(8,128)(2,1)}, bf16[128,512]{1,0:T(8,128)(2,1)S(1)}, u32[]{:S(2)}, u32[]{:S(2)}) collective-permute-start(bf16[128,512]{1,0:T(8,128)(2,1)} %bitcast.11), channel_id=1, source_target_pairs={{0,130},{128,0},{2,128},{130,2},{1,131},{129,1},{3,129},{131,3},{4... | collective-permute-start | bytes 393224 | tf_op jit(solution)/shard_map/ppermute | solution.py:250
  6.8 12.0 %collective-permute-start = (bf16[128,512]{1,0:T(8,128)(2,1)}, bf16[128,512]{1,0:T(8,128)(2,1)S(1)}, u32[]{:S(2)}, u32[]{:S(2)}) collective-permute-start(bf16[128,512]{1,0:T(8,128)(2,1)} %bitcast.12), channel_id=1, source_target_pairs={{0,1},{1,0},{2,3},{3,2},{4,5},{5,4},{6,7},{7,6},{8,9},{9,8},{10,11... | collective-permute-start | bytes 393224 | tf_op jit(solution)/shard_map/ppermute | solution.py:28
  7.8 12.4 %collective-permute-start.8 = (bf16[128,512]{1,0:T(8,128)(2,1)}, bf16[128,512]{1,0:T(8,128)(2,1)S(1)}, u32[]{:S(2)}, u32[]{:S(2)}) collective-permute-start(bf16[128,512]{1,0:T(8,128)(2,1)} %bitcast.17), channel_id=1, source_target_pairs={{0,130},{128,0},{2,128},{130,2},{1,131},{129,1},{3,129},{131,3},{4... | collective-permute-start | bytes 393224 | tf_op jit(solution)/shard_map/ppermute | solution.py:250
  10.4 12.1 %collective-permute-start.11 = (bf16[128,512]{1,0:T(8,128)(2,1)}, bf16[128,512]{1,0:T(8,128)(2,1)S(1)}, u32[]{:S(2)}, u32[]{:S(2)}) collective-permute-start(bf16[128,512]{1,0:T(8,128)(2,1)} %bitcast.18), channel_id=1, source_target_pairs={{0,128},{128,2},{2,130},{130,0},{1,129},{129,3},{3,131},{131,1},{4... | collective-permute-start | bytes 393224 | tf_op jit(solution)/shard_map/ppermute | solution.py:250
  10.8 14.0 %collective-permute-start.2 = (bf16[128,512]{1,0:T(8,128)(2,1)S(1)}, bf16[128,512]{1,0:T(8,128)(2,1)S(1)}, u32[]{:S(2)}, u32[]{:S(2)}) collective-permute-start(bf16[128,512]{1,0:T(8,128)(2,1)S(1)} %collective-permute-done.1.refs_0_.refs_4_), channel_id=1, source_target_pairs={{0,128},{128,2},{2,130},{130,0},{1,129},{129,3},{3,131},{131,1},{4... | collective-permute-start | bytes 393224 | tf_op jit(solution)/shard_map/ppermute | solution.py:250
  17.4 9.3 %collective-permute-start.6 = (bf16[128,512]{1,0:T(8,128)(2,1)S(1)}, bf16[128,512]{1,0:T(8,128)(2,1)S(1)}, u32[]{:S(2)}, u32[]{:S(2)}) collective-permute-start(bf16[128,512]{1,0:T(8,128)(2,1)S(1)} %collective-permute-done.5.refs_2_.refs_6_), channel_id=1, source_target_pairs={{0,1},{1,0},{2,3},{3,2},{4,5},{5,4},{6,7},{7,6},{8,9},{9,8},{10,11... | collective-permute-start | bytes 393224 | tf_op jit(solution)/shard_map/ppermute | solution.py:28
  18.9 7.8 %collective-permute-start.4 = (bf16[128,512]{1,0:T(8,128)(2,1)S(1)}, bf16[128,512]{1,0:T(8,128)(2,1)S(1)}, u32[]{:S(2)}, u32[]{:S(2)}) collective-permute-start(bf16[128,512]{1,0:T(8,128)(2,1)S(1)} %collective-permute-done.1.refs_0_.refs_4_), channel_id=1, source_target_pairs={{0,1},{1,0},{2,3},{3,2},{4,5},{5,4},{6,7},{7,6},{8,9},{9,8},{10,11... | collective-permute-start | bytes 393224 | tf_op jit(solution)/shard_map/ppermute | solution.py:28
  20.2 8.5 %collective-permute-start.9 = (bf16[128,512]{1,0:T(8,128)(2,1)S(1)}, bf16[128,512]{1,0:T(8,128)(2,1)S(1)}, u32[]{:S(2)}, u32[]{:S(2)}) collective-permute-start(bf16[128,512]{1,0:T(8,128)(2,1)S(1)} %collective-permute-done.8.refs_14_), channel_id=1, source_target_pairs={{0,130},{128,0},{2,128},{130,2},{1,131},{129,1},{3,129},{131,3},{4... | collective-permute-start | bytes 393224 | tf_op jit(solution)/shard_map/ppermute | solution.py:250
  22.5 15.3 %collective-permute-start.7 = (bf16[128,512]{1,0:T(8,128)(2,1)}, bf16[128,512]{1,0:T(8,128)(2,1)S(1)}, u32[]{:S(2)}, u32[]{:S(2)}) collective-permute-start(bf16[128,512]{1,0:T(8,128)(2,1)} %bitcast.19), channel_id=1, source_target_pairs={{0,1},{1,0},{2,3},{3,2},{4,5},{5,4},{6,7},{7,6},{8,9},{9,8},{10,11... | collective-permute-start | bytes 393224 | tf_op jit(solution)/shard_map/ppermute | solution.py:28
  24.9 10.3 %collective-permute-start.3 = (bf16[128,512]{1,0:T(8,128)(2,1)S(1)}, bf16[128,512]{1,0:T(8,128)(2,1)S(1)}, u32[]{:S(2)}, u32[]{:S(2)}) collective-permute-start(bf16[128,512]{1,0:T(8,128)(2,1)S(1)} %collective-permute-done.2.refs_2_), channel_id=1, source_target_pairs={{0,1},{1,0},{2,3},{3,2},{4,5},{5,4},{6,7},{7,6},{8,9},{9,8},{10,11... | collective-permute-start | bytes 393224 | tf_op jit(solution)/shard_map/ppermute | solution.py:28
  26.7 11.2 %collective-permute-start.13 = (bf16[128,512]{1,0:T(8,128)(2,1)S(1)}, bf16[128,512]{1,0:T(8,128)(2,1)S(1)}, u32[]{:S(2)}, u32[]{:S(2)}) collective-permute-start(bf16[128,512]{1,0:T(8,128)(2,1)S(1)} %collective-permute-done.8.refs_14_), channel_id=1, source_target_pairs={{0,1},{1,0},{2,3},{3,2},{4,5},{5,4},{6,7},{7,6},{8,9},{9,8},{10,11... | collective-permute-start | bytes 393224 | tf_op jit(solution)/shard_map/ppermute | solution.py:28
  26.7 11.2 %collective-permute-start.12 = (bf16[128,512]{1,0:T(8,128)(2,1)S(1)}, bf16[128,512]{1,0:T(8,128)(2,1)S(1)}, u32[]{:S(2)}, u32[]{:S(2)}) collective-permute-start(bf16[128,512]{1,0:T(8,128)(2,1)S(1)} %collective-permute-done.11.refs_12_), channel_id=1, source_target_pairs={{0,1},{1,0},{2,3},{3,2},{4,5},{5,4},{6,7},{7,6},{8,9},{9,8},{10,11... | collective-permute-start | bytes 393224 | tf_op jit(solution)/shard_map/ppermute | solution.py:28
  28.7 9.2 %collective-permute-start.10 = (bf16[128,512]{1,0:T(8,128)(2,1)S(1)}, bf16[128,512]{1,0:T(8,128)(2,1)S(1)}, u32[]{:S(2)}, u32[]{:S(2)}) collective-permute-start(bf16[128,512]{1,0:T(8,128)(2,1)S(1)} %collective-permute-done.9.refs_10_), channel_id=1, source_target_pairs={{0,1},{1,0},{2,3},{3,2},{4,5},{5,4},{6,7},{7,6},{8,9},{9,8},{10,11... | collective-permute-start | bytes 393224 | tf_op jit(solution)/shard_map/ppermute | solution.py:28
  30.0 2.5 %copy-start.1 = (f32[128,128]{1,0:T(8,128)S(1)}, f32[128,128]{1,0:T(8,128)}, u32[]{:S(2)}) copy-start(f32[128,128]{1,0:T(8,128)} %constant.34.clone.refs_8_) | copy-start | bytes 196612
  30.0 2.5 %copy-start.2 = (f32[128,128]{1,0:T(8,128)S(1)}, f32[128,128]{1,0:T(8,128)}, u32[]{:S(2)}) copy-start(f32[128,128]{1,0:T(8,128)} %constant.33.clone.refs_7_) | copy-start | bytes 196612
  32.4 2.7 %copy-start = (bf16[1,128,512]{2,1,0:T(8,128)(2,1)S(1)}, bf16[1,128,512]{2,1,0:T(8,128)(2,1)}, u32[]{:S(2)}) copy-start(bf16[1,128,512]{2,1,0:T(8,128)(2,1)} %param.8) | copy-start | bytes 393220
  32.5 5.4 %copy-start.3 = (bf16[1,128,512]{2,1,0:T(8,128)(2,1)S(1)}, bf16[1,128,512]{2,1,0:T(8,128)(2,1)}, u32[]{:S(2)}) copy-start(bf16[1,128,512]{2,1,0:T(8,128)(2,1)} %param.9) | copy-start | bytes 393220

commit v2 on v1

--- a/solution.py
+++ b/solution.py
@@ -45,13 +45,18 @@
 def kernel_call(body, outs, ins, scratch=(), vmem_mib=20, far=()):
     ins = [pltpu.with_memory_space_constraint(a, pltpu.HBM) if i in far else a for i, a in enumerate(ins)]
     hbm = pl.BlockSpec(memory_space=pltpu.HBM)
-    smem = pl.BlockSpec(memory_space=pltpu.SMEM)
     vmem = pl.BlockSpec(memory_space=pltpu.VMEM)
+
+    def with_place(*refs):
+        zb, za, x, y = (lax.axis_index(a) for a in SEQ)
+        place = ((zb * lax.axis_size("za") + za) * lax.axis_size("x") + x) * lax.axis_size("y") + y
+        body((lax.axis_index("h"), lax.axis_index("c"), zb, place), *refs)
+
     return pl.pallas_call(
-        body,
+        with_place,
         out_shape=outs,
         in_specs=[
-            hbm if i in far else smem if a.dtype == jnp.int32 else vmem for i, a in enumerate(ins)
+            hbm if i in far else vmem for i in range(len(ins))
         ],
         out_specs=jax.tree.map(lambda _: vmem, outs),
         scratch_shapes=scratch,
@@ -198,12 +203,15 @@
     tall = both // 2
     straight = at[2] == 0
     for s in range(seqs):
-        wide[pl.ds(s * both, both), :] = got[s].astype(jnp.float32)
+        for t in range(both // 8):
+            wide[pl.ds((t * seqs + s) * 8, 8), :] = got[s, t * 8 : t * 8 + 8, :].astype(jnp.float32)
 
     def rows_of(r):
-        found = [
-            wide[pl.ds(r + k * tall, seqs, stride=both), :].astype(jnp.bfloat16) for k in range(2)
-        ]
+        found = []
+        for k in range(2):
+            t, rest = divmod(r + k * tall, 8)
+            rows = wide[pl.ds(t * seqs * 8 + rest, seqs, stride=8), :]
+            found.append(rows.astype(jnp.bfloat16))
         return jnp.concatenate(
             [jnp.where(straight, found[0], found[1]), jnp.where(straight, found[1], found[0])], axis=0
         )
@@ -236,8 +244,6 @@
     shape = jax.ShapeDtypeStruct
     length, part = states.shape[1:]
     states, cotangent = states[0], cotangent[0]
-    axes = (lax.axis_index("h"), lax.axis_index("c"), lax.axis_index("zb"), lax.axis_index(SEQ))
-    at = jnp.stack(axes).astype(jnp.int32)
     blocks = lax.axis_size(NEAR)
     seqs = 2 * blocks
     tall = (part + LANES) * (2 * part) // (LANES * blocks)
@@ -267,9 +273,9 @@
             shape(dims, bf16)
             for dims in ((wq.shape[0], width), wk.shape, wv.shape, (width, wo.shape[1]))
         ),
-        (at, wq, wk, wv, wo),
+        (wq, wk, wv, wo),
         (pltpu.SemaphoreType.DMA((4,)),),
-        far=(1, 2, 3, 4),
+        far=(0, 1, 2, 3),
     )
 
     def attention(partner, parts):
@@ -279,7 +285,7 @@
                 shape((length, width), bf16),
                 shape((width // HEAD_DIM * length, length), bf16),
             ),
-            (at, *parts, wq, wk, wv, cos, sine),
+            (*parts, wq, wk, wv, cos, sine),
         )
 
     partner_found = attention(True, s_parts[4:])
@@ -287,19 +293,19 @@
     sent = kernel_call(
         blocks_body,
         shape((blocks, 2 * tall, LANES), bf16),
-        (at, *s_parts, *c_parts, wo, *own_found, *partner_found),
+        (*s_parts, *c_parts, wo, *own_found, *partner_found),
     )
     got = lax.all_to_all(sent, NEAR, 0, 0, tiled=True)
     copies = lax.axis_size(TP)
     rows = kernel_call(
         share_body,
         shape((seqs * copies, 2 * seqs), f32),
-        (at, got),
+        (got,),
         (pltpu.VMEM((seqs * tall, LANES), f32),),
     )
     rows = rows.reshape(seqs * copies, 1, 2 * seqs)
     got = lax.all_to_all(rows, EVERY, 0, 0, tiled=True).reshape(seqs * copies, 2 * seqs)
-    return kernel_call(final_body, shape((1, seqs), f32), (at, got))
+    return kernel_call(final_body, shape((1, seqs), f32), (got,))
 
 
 def solution(mesh):

time: 108 us -> 103 us (0.954)
  Pallas kernels: 16.1 us -> 10.5 us
    pallas_call x6, Pallas kernels: 16.1 us -> 10.5 us  [kernel_call(): pl.pallas_call(with_place, out_shape=outs, in_specs=[hbm if i in far else...]
  transfers between devices with their start and end apart: 14 -> 14, of which waited for: 5 -> 5; matrix products, arithmetic and copies ran while one was open for 0% -> 0% of each run, Pallas kernels for 7% -> 6%
where the time goes in v2:
time: 103 us; the launch traced here: 102 us
  blocking collectives  61.9 us (60%)
  starting transfers between devices  23.7 us (23%)
  Pallas kernels  10.5 us (10%)
  waiting for transfers between devices  6.23 us (6%)
    all_to_all x1, blocking collectives, on_device(): got = lax.all_to_all(sent, NEAR, 0, 0, tiled=True)  39.7 us
    all_to_all x1, blocking collectives, on_device(): lax.all_to_all(rows, EVERY, 0, 0, tiled=True)  22.1 us
    ppermute x6, starting transfers between devices, moved(): return lax.ppermute(piece, ('zb', 'h'), around(step))  16.5 us
    pallas_call x6, Pallas kernels, kernel_call(): pl.pallas_call(with_place, out_shape=outs, in_specs=[hbm if i in far else...  10.5 us
    ppermute x8, starting transfers between devices, swapped(): return lax.ppermute(value, axis, SWAP)  7.21 us
    ppermute x6, waiting for transfers between devices, moved(): return lax.ppermute(piece, ('zb', 'h'), around(step))  6.21 us
  transfers between devices with their start and end apart: 14, of which 5 were waited for; matrix products, arithmetic and copies ran while one was open for 0% of the time, Pallas kernels for 6%

profile of v2, /device:TPU:1, one launch (start us, length us, event | category | flops | bytes accessed | tf_op | source)
XLA Modules:
  0.0 102.4 jit_solution(2960114395892094559)
XLA Ops:
  0.0 3.8 %collective-permute-start.1 = (bf16[128,512]{1,0:T(8,128)(2,1)}, bf16[128,512]{1,0:T(8,128)(2,1)S(1)}, u32[]{:S(2)}, u32[]{:S(2)}) collective-permute-start(bf16[128,512]{1,0:T(8,128)(2,1)} %bitcast.7), channel_id=1, source_target_pairs={{0,128},{128,2},{2,130},{130,0},{1,129},{129,3},{3,131},{131,1},{4... | collective-permute-start | bytes 393224 | tf_op jit(solution)/shard_map/ppermute | solution.py:256
  3.8 3.0 %collective-permute-start.5 = (bf16[128,512]{1,0:T(8,128)(2,1)}, bf16[128,512]{1,0:T(8,128)(2,1)S(1)}, u32[]{:S(2)}, u32[]{:S(2)}) collective-permute-start(bf16[128,512]{1,0:T(8,128)(2,1)} %bitcast.8), channel_id=1, source_target_pairs={{0,130},{128,0},{2,128},{130,2},{1,131},{129,1},{3,129},{131,3},{4... | collective-permute-start | bytes 393224 | tf_op jit(solution)/shard_map/ppermute | solution.py:256
  6.8 1.0 collective-permute-start
  7.8 2.6 %collective-permute-start.8 = (bf16[128,512]{1,0:T(8,128)(2,1)}, bf16[128,512]{1,0:T(8,128)(2,1)S(1)}, u32[]{:S(2)}, u32[]{:S(2)}) collective-permute-start(bf16[128,512]{1,0:T(8,128)(2,1)} %bitcast.13), channel_id=1, source_target_pairs={{0,130},{128,0},{2,128},{130,2},{1,131},{129,1},{3,129},{131,3},{4... | collective-permute-start | bytes 393224 | tf_op jit(solution)/shard_map/ppermute | solution.py:256
  10.4 0.4 collective-permute-done.1.refs_0_.refs_4_
  10.8 4.6 %collective-permute-start.2 = (bf16[128,512]{1,0:T(8,128)(2,1)S(1)}, bf16[128,512]{1,0:T(8,128)(2,1)S(1)}, u32[]{:S(2)}, u32[]{:S(2)}) collective-permute-start(bf16[128,512]{1,0:T(8,128)(2,1)S(1)} %collective-permute-done.1.refs_0_.refs_4_), channel_id=1, source_target_pairs={{0,128},{128,2},{2,130},{130,0},{1,129},{129,3},{3,131},{131,1},{4... | collective-permute-start | bytes 393224 | tf_op jit(solution)/shard_map/ppermute | solution.py:256
  15.5 1.9 %collective-permute-done.5.refs_2_.refs_6_ = bf16[128,512]{1,0:T(8,128)(2,1)S(1)} collective-permute-done((bf16[128,512]{1,0:T(8,128)(2,1)}, bf16[128,512]{1,0:T(8,128)(2,1)S(1)}, u32[]{:S(2)}, u32[]{:S(2)}) %collective-permute-start.5) | collective-permute-done | bytes 131104 | tf_op jit(solution)/shard_map/ppermute | solution.py:256
  17.4 1.5 %collective-permute-start.6 = (bf16[128,512]{1,0:T(8,128)(2,1)S(1)}, bf16[128,512]{1,0:T(8,128)(2,1)S(1)}, u32[]{:S(2)}, u32[]{:S(2)}) collective-permute-start(bf16[128,512]{1,0:T(8,128)(2,1)S(1)} %collective-permute-done.5.refs_2_.refs_6_), channel_id=1, source_target_pairs={{0,1},{1,0},{2,3},{3,2},{4,5},{5,4},{6,7},{7,6},{8,9},{9,8},{10,11... | collective-permute-start | bytes 393224 | tf_op jit(solution)/shard_map/ppermute | solution.py:28
  18.9 1.3 %collective-permute-done.8.refs_14_ = bf16[128,512]{1,0:T(8,128)(2,1)S(1)} collective-permute-done((bf16[128,512]{1,0:T(8,128)(2,1)}, bf16[128,512]{1,0:T(8,128)(2,1)S(1)}, u32[]{:S(2)}, u32[]{:S(2)}) %collective-permute-start.8) | collective-permute-done | bytes 131104 | tf_op jit(solution)/shard_map/ppermute | solution.py:256
  20.2 2.4 %collective-permute-start.9 = (bf16[128,512]{1,0:T(8,128)(2,1)S(1)}, bf16[128,512]{1,0:T(8,128)(2,1)S(1)}, u32[]{:S(2)}, u32[]{:S(2)}) collective-permute-start(bf16[128,512]{1,0:T(8,128)(2,1)S(1)} %collective-permute-done.8.refs_14_), channel_id=1, source_target_pairs={{0,130},{128,0},{2,128},{130,2},{1,131},{129,1},{3,129},{131,3},{4... | collective-permute-start | bytes 393224 | tf_op jit(solution)/shard_map/ppermute | solution.py:256
  22.5 1.3 %collective-permute-start.7 = (bf16[128,512]{1,0:T(8,128)(2,1)}, bf16[128,512]{1,0:T(8,128)(2,1)S(1)}, u32[]{:S(2)}, u32[]{:S(2)}) collective-permute-start(bf16[128,512]{1,0:T(8,128)(2,1)} %bitcast.15), channel_id=1, source_target_pairs={{0,1},{1,0},{2,3},{3,2},{4,5},{5,4},{6,7},{7,6},{8,9},{9,8},{10,11... | collective-permute-start | bytes 393224 | tf_op jit(solution)/shard_map/ppermute | solution.py:28
  23.8 1.1 %collective-permute-done.2.refs_2_ = bf16[128,512]{1,0:T(8,128)(2,1)S(1)} collective-permute-done((bf16[128,512]{1,0:T(8,128)(2,1)S(1)}, bf16[128,512]{1,0:T(8,128)(2,1)S(1)}, u32[]{:S(2)}, u32[]{:S(2)}) %collective-permute-start.2) | collective-permute-done | bytes 131104 | tf_op jit(solution)/shard_map/ppermute | solution.py:256
  24.9 1.8 %collective-permute-start.3 = (bf16[128,512]{1,0:T(8,128)(2,1)S(1)}, bf16[128,512]{1,0:T(8,128)(2,1)S(1)}, u32[]{:S(2)}, u32[]{:S(2)}) collective-permute-start(bf16[128,512]{1,0:T(8,128)(2,1)S(1)} %collective-permute-done.2.refs_2_), channel_id=1, source_target_pairs={{0,1},{1,0},{2,3},{3,2},{4,5},{5,4},{6,7},{7,6},{8,9},{9,8},{10,11... | collective-permute-start | bytes 393224 | tf_op jit(solution)/shard_map/ppermute | solution.py:28
  26.7 0.5 collective-permute-start.12
  27.2 1.5 %collective-permute-done.9.refs_10_ = bf16[128,512]{1,0:T(8,128)(2,1)S(1)} collective-permute-done((bf16[128,512]{1,0:T(8,128)(2,1)S(1)}, bf16[128,512]{1,0:T(8,128)(2,1)S(1)}, u32[]{:S(2)}, u32[]{:S(2)}) %collective-permute-start.9) | collective-permute-done | bytes 131104 | tf_op jit(solution)/shard_map/ppermute | solution.py:256
  28.7 1.2 %collective-permute-start.10 = (bf16[128,512]{1,0:T(8,128)(2,1)S(1)}, bf16[128,512]{1,0:T(8,128)(2,1)S(1)}, u32[]{:S(2)}, u32[]{:S(2)}) collective-permute-start(bf16[128,512]{1,0:T(8,128)(2,1)S(1)} %collective-permute-done.9.refs_10_), channel_id=1, source_target_pairs={{0,1},{1,0},{2,3},{3,2},{4,5},{5,4},{6,7},{7,6},{8,9},{9,8},{10,11... | collective-permute-start | bytes 393224 | tf_op jit(solution)/shard_map/ppermute | solution.py:28
  29.9 1.9 %shard_map.82 = (bf16[2048,256]{1,0:T(8,128)(2,1)S(1)}, bf16[2048,128]{1,0:T(8,128)(2,1)S(1)}, bf16[2048,128]{1,0:T(8,128)(2,1)S(1)}, bf16[256,2048]{1,0:T(8,128)(2,1)S(1)}) custom-call(bf16[2048,512]{1,0:T(8,128)(2,1)} %refs_0_.1, bf16[2048,128]{1,0:T(8,128)(2,1)} %refs_1_.1, bf16[2048,128]{1,0:T(8,128)(2,1)} %refs_2_.1, bf16[512,2048]{1,0:T(8,128)(2,1)} %refs_3_.1), custom_call_target="tpu_custom_call" | custom-call | tf_op jit(solution)/shard_map/pallas_call | solution.py:55
  31.8 2.1 %shard_map.84 = (bf16[128,256]{1,0:T(8,128)(2,1)S(1)}, bf16[512,128]{1,0:T(8,128)(2,1)S(1)}) custom-call(bf16[128,512]{1,0:T(8,128)(2,1)S(1)} %collective-permute-done.1.refs_0_.refs_4_, bf16[128,512]{1,0:T(8,128)(2,1)S(1)} %collective-permute-done.4.refs_1_.refs_5_, bf16[128,512]{1,0:T(8,128)(2,1)S(1)} %collective-permute-done.5.refs_2_.refs_6_, ...), custom_call_target="tpu_custom_call" | custom-call | tf_op jit(solution)/shard_map/pallas_call | solution.py:55
  34.0 2.1 %shard_map.83 = (bf16[128,256]{1,0:T(8,128)(2,1)S(1)}, bf16[512,128]{1,0:T(8,128)(2,1)S(1)}) custom-call(bf16[128,512]{1,0:T(8,128)(2,1)S(1)} %bitcast.10, bf16[128,512]{1,0:T(8,128)(2,1)S(1)} %collective-permute-done.refs_1_, bf16[128,512]{1,0:T(8,128)(2,1)S(1)} %collective-permute-done.2.refs_2_, bf16[128,512]{1,0:T(8,128)(2,1)S(1)} %collective-permute-done.3.refs_3_, ...), custom_call_target="tpu_custom_call" | custom-call | tf_op jit(solution)/shard_map/pallas_call | solution.py:55
  36.2 2.2 %shard_map.85 = bf16[32,320,128]{2,1,0:T(8,128)(2,1)S(1)} custom-call(bf16[128,512]{1,0:T(8,128)(2,1)S(1)} %bitcast.11, bf16[128,512]{1,0:T(8,128)(2,1)S(1)} %collective-permute-done.refs_1_, bf16[128,512]{1,0:T(8,128)(2,1)S(1)} %collective-permute-done.2.refs_2_, bf16[128,512]{1,0:T(8,128)(2,1)S(1)} %collective-permute-done.3.refs_3_, ...), custom_call_target="tpu_custom_call" | custom-call | tf_op jit(solution)/shard_map/pallas_call | solution.py:55
  38.4 39.7 %all_to_all.10.refs_0_ = bf16[32,320,128]{2,1,0:T(8,128)(2,1)S(1)} all-to-all(bf16[32,320,128]{2,1,0:T(8,128)(2,1)S(1)} %shard_map.85), channel_id=1, replica_groups=mesh['zb'=2,'za'=2,'x'=4,'y'=4,'h'=2,'c'=2] {'za','x','y'}, dimensions={0} | all-to-all | bytes 5242880 | tf_op jit(solution)/shard_map/all_to_all | solution.py:298
  78.1 1.5 %shard_map.86 = f32[256,128]{1,0:T(8,128)S(1)} custom-call(bf16[32,320,128]{2,1,0:T(8,128)(2,1)S(1)} %all_to_all.10.refs_0_), custom_call_target="tpu_custom_call" | custom-call | tf_op jit(solution)/shard_map/pallas_call | solution.py:55
  79.6 22.1 %all_to_all.11 = f32[256,1,128]{2,1,0:T(1,128)S(1)} all-to-all(f32[256,1,128]{2,1,0:T(1,128)S(1)} %bitcast.12), channel_id=1, replica_groups=mesh['zb'=2,'za'=2,'x'=4,'y'=4,'h'=2,'c'=2] {'zb','za','x','y','h','c'}, dimensions={0} | all-to-all | bytes 262144 | tf_op jit(solution)/shard_map/all_to_all | solution.py:307
  101.8 0.6 shard_map.87
  (20 shorter events, 0.1 us)
Async XLA Ops:
  0.0 10.8 %collective-permute-start.1 = (bf16[128,512]{1,0:T(8,128)(2,1)}, bf16[128,512]{1,0:T(8,128)(2,1)S(1)}, u32[]{:S(2)}, u32[]{:S(2)}) collective-permute-start(bf16[128,512]{1,0:T(8,128)(2,1)} %bitcast.7), channel_id=1, source_target_pairs={{0,128},{128,2},{2,130},{130,0},{1,129},{129,3},{3,131},{131,1},{4... | collective-permute-start | bytes 393224 | tf_op jit(solution)/shard_map/ppermute | solution.py:256
  3.8 13.6 %collective-permute-start.5 = (bf16[128,512]{1,0:T(8,128)(2,1)}, bf16[128,512]{1,0:T(8,128)(2,1)S(1)}, u32[]{:S(2)}, u32[]{:S(2)}) collective-permute-start(bf16[128,512]{1,0:T(8,128)(2,1)} %bitcast.8), channel_id=1, source_target_pairs={{0,130},{128,0},{2,128},{130,2},{1,131},{129,1},{3,129},{131,3},{4... | collective-permute-start | bytes 393224 | tf_op jit(solution)/shard_map/ppermute | solution.py:256
  6.8 12.0 %collective-permute-start = (bf16[128,512]{1,0:T(8,128)(2,1)}, bf16[128,512]{1,0:T(8,128)(2,1)S(1)}, u32[]{:S(2)}, u32[]{:S(2)}) collective-permute-start(bf16[128,512]{1,0:T(8,128)(2,1)} %bitcast.9), channel_id=1, source_target_pairs={{0,1},{1,0},{2,3},{3,2},{4,5},{5,4},{6,7},{7,6},{8,9},{9,8},{10,11... | collective-permute-start | bytes 393224 | tf_op jit(solution)/shard_map/ppermute | solution.py:28
  7.8 24.0 %copy-start.1 = (f32[128,128]{1,0:T(8,128)S(1)}, f32[128,128]{1,0:T(8,128)}, u32[]{:S(2)}) copy-start(f32[128,128]{1,0:T(8,128)} %constant.5.clone.refs_8_) | copy-start | bytes 196612
  7.8 24.0 %copy-start.2 = (f32[128,128]{1,0:T(8,128)S(1)}, f32[128,128]{1,0:T(8,128)}, u32[]{:S(2)}) copy-start(f32[128,128]{1,0:T(8,128)} %constant.4.clone.refs_7_) | copy-start | bytes 196612
  7.8 12.4 %collective-permute-start.8 = (bf16[128,512]{1,0:T(8,128)(2,1)}, bf16[128,512]{1,0:T(8,128)(2,1)S(1)}, u32[]{:S(2)}, u32[]{:S(2)}) collective-permute-start(bf16[128,512]{1,0:T(8,128)(2,1)} %bitcast.13), channel_id=1, source_target_pairs={{0,130},{128,0},{2,128},{130,2},{1,131},{129,1},{3,129},{131,3},{4... | collective-permute-start | bytes 393224 | tf_op jit(solution)/shard_map/ppermute | solution.py:256
  10.4 12.1 %collective-permute-start.11 = (bf16[128,512]{1,0:T(8,128)(2,1)}, bf16[128,512]{1,0:T(8,128)(2,1)S(1)}, u32[]{:S(2)}, u32[]{:S(2)}) collective-permute-start(bf16[128,512]{1,0:T(8,128)(2,1)} %bitcast.14), channel_id=1, source_target_pairs={{0,128},{128,2},{2,130},{130,0},{1,129},{129,3},{3,131},{131,1},{4... | collective-permute-start | bytes 393224 | tf_op jit(solution)/shard_map/ppermute | solution.py:256
  10.8 14.0 %collective-permute-start.2 = (bf16[128,512]{1,0:T(8,128)(2,1)S(1)}, bf16[128,512]{1,0:T(8,128)(2,1)S(1)}, u32[]{:S(2)}, u32[]{:S(2)}) collective-permute-start(bf16[128,512]{1,0:T(8,128)(2,1)S(1)} %collective-permute-done.1.refs_0_.refs_4_), channel_id=1, source_target_pairs={{0,128},{128,2},{2,130},{130,0},{1,129},{129,3},{3,131},{131,1},{4... | collective-permute-start | bytes 393224 | tf_op jit(solution)/shard_map/ppermute | solution.py:256
  17.4 9.3 %collective-permute-start.6 = (bf16[128,512]{1,0:T(8,128)(2,1)S(1)}, bf16[128,512]{1,0:T(8,128)(2,1)S(1)}, u32[]{:S(2)}, u32[]{:S(2)}) collective-permute-start(bf16[128,512]{1,0:T(8,128)(2,1)S(1)} %collective-permute-done.5.refs_2_.refs_6_), channel_id=1, source_target_pairs={{0,1},{1,0},{2,3},{3,2},{4,5},{5,4},{6,7},{7,6},{8,9},{9,8},{10,11... | collective-permute-start | bytes 393224 | tf_op jit(solution)/shard_map/ppermute | solution.py:28
  18.9 7.8 %collective-permute-start.4 = (bf16[128,512]{1,0:T(8,128)(2,1)S(1)}, bf16[128,512]{1,0:T(8,128)(2,1)S(1)}, u32[]{:S(2)}, u32[]{:S(2)}) collective-permute-start(bf16[128,512]{1,0:T(8,128)(2,1)S(1)} %collective-permute-done.1.refs_0_.refs_4_), channel_id=1, source_target_pairs={{0,1},{1,0},{2,3},{3,2},{4,5},{5,4},{6,7},{7,6},{8,9},{9,8},{10,11... | collective-permute-start | bytes 393224 | tf_op jit(solution)/shard_map/ppermute | solution.py:28
  20.2 8.5 %collective-permute-start.9 = (bf16[128,512]{1,0:T(8,128)(2,1)S(1)}, bf16[128,512]{1,0:T(8,128)(2,1)S(1)}, u32[]{:S(2)}, u32[]{:S(2)}) collective-permute-start(bf16[128,512]{1,0:T(8,128)(2,1)S(1)} %collective-permute-done.8.refs_14_), channel_id=1, source_target_pairs={{0,130},{128,0},{2,128},{130,2},{1,131},{129,1},{3,129},{131,3},{4... | collective-permute-start | bytes 393224 | tf_op jit(solution)/shard_map/ppermute | solution.py:256
  22.5 13.6 %collective-permute-start.7 = (bf16[128,512]{1,0:T(8,128)(2,1)}, bf16[128,512]{1,0:T(8,128)(2,1)S(1)}, u32[]{:S(2)}, u32[]{:S(2)}) collective-permute-start(bf16[128,512]{1,0:T(8,128)(2,1)} %bitcast.15), channel_id=1, source_target_pairs={{0,1},{1,0},{2,3},{3,2},{4,5},{5,4},{6,7},{7,6},{8,9},{9,8},{10,11... | collective-permute-start | bytes 393224 | tf_op jit(solution)/shard_map/ppermute | solution.py:28
  24.9 9.1 %collective-permute-start.3 = (bf16[128,512]{1,0:T(8,128)(2,1)S(1)}, bf16[128,512]{1,0:T(8,128)(2,1)S(1)}, u32[]{:S(2)}, u32[]{:S(2)}) collective-permute-start(bf16[128,512]{1,0:T(8,128)(2,1)S(1)} %collective-permute-done.2.refs_2_), channel_id=1, source_target_pairs={{0,1},{1,0},{2,3},{3,2},{4,5},{5,4},{6,7},{7,6},{8,9},{9,8},{10,11... | collective-permute-start | bytes 393224 | tf_op jit(solution)/shard_map/ppermute | solution.py:28
  26.7 9.5 %collective-permute-start.13 = (bf16[128,512]{1,0:T(8,128)(2,1)S(1)}, bf16[128,512]{1,0:T(8,128)(2,1)S(1)}, u32[]{:S(2)}, u32[]{:S(2)}) collective-permute-start(bf16[128,512]{1,0:T(8,128)(2,1)S(1)} %collective-permute-done.8.refs_14_), channel_id=1, source_target_pairs={{0,1},{1,0},{2,3},{3,2},{4,5},{5,4},{6,7},{7,6},{8,9},{9,8},{10,11... | collective-permute-start | bytes 393224 | tf_op jit(solution)/shard_map/ppermute | solution.py:28
  26.7 9.5 %collective-permute-start.12 = (bf16[128,512]{1,0:T(8,128)(2,1)S(1)}, bf16[128,512]{1,0:T(8,128)(2,1)S(1)}, u32[]{:S(2)}, u32[]{:S(2)}) collective-permute-start(bf16[128,512]{1,0:T(8,128)(2,1)S(1)} %collective-permute-done.11.refs_12_), channel_id=1, source_target_pairs={{0,1},{1,0},{2,3},{3,2},{4,5},{5,4},{6,7},{7,6},{8,9},{9,8},{10,11... | collective-permute-start | bytes 393224 | tf_op jit(solution)/shard_map/ppermute | solution.py:28
  28.7 7.4 %collective-permute-start.10 = (bf16[128,512]{1,0:T(8,128)(2,1)S(1)}, bf16[128,512]{1,0:T(8,128)(2,1)S(1)}, u32[]{:S(2)}, u32[]{:S(2)}) collective-permute-start(bf16[128,512]{1,0:T(8,128)(2,1)S(1)} %collective-permute-done.9.refs_10_), channel_id=1, source_target_pairs={{0,1},{1,0},{2,3},{3,2},{4,5},{5,4},{6,7},{7,6},{8,9},{9,8},{10,11... | collective-permute-start | bytes 393224 | tf_op jit(solution)/shard_map/ppermute | solution.py:28
  31.8 2.2 %copy-start = (bf16[1,128,512]{2,1,0:T(8,128)(2,1)S(1)}, bf16[1,128,512]{2,1,0:T(8,128)(2,1)}, u32[]{:S(2)}) copy-start(bf16[1,128,512]{2,1,0:T(8,128)(2,1)} %param.8) | copy-start | bytes 393220
  31.8 4.3 %copy-start.3 = (bf16[1,128,512]{2,1,0:T(8,128)(2,1)S(1)}, bf16[1,128,512]{2,1,0:T(8,128)(2,1)}, u32[]{:S(2)}) copy-start(bf16[1,128,512]{2,1,0:T(8,128)(2,1)} %param.9) | copy-start | bytes 393220

commit v3 on v2

--- a/solution.py
+++ b/solution.py
@@ -83,7 +83,9 @@
 
 
 def own_quarters(parts):
-    return [part[...] for part in parts]
+    values = [part[...] for part in parts]
+    far = [jnp.concatenate([values[2 + k], values[4 + k]], axis=0) for k in range(2)]
+    return values[:2] + far
 
 
 def partner_quarters(at, parts):
@@ -158,11 +160,11 @@
 
 
 def blocks_body(at, *refs):
-    s_refs, c_refs = refs[:8], refs[8:16]
-    wo, attended_own, probs_own, attended_partner, probs_partner, blocks = refs[16:]
+    s_refs, c_refs = refs[:10], refs[10:20]
+    wo, attended_own, probs_own, attended_partner, probs_partner, blocks = refs[20:]
     attended, probs = (attended_own, attended_partner), (probs_own, probs_partner)
-    states = list(zip(own_quarters(s_refs[:4]), partner_quarters(at, s_refs[4:])))
-    cots = list(zip(own_quarters(c_refs[:4]), partner_quarters(at, c_refs[4:])))
+    states = list(zip(own_quarters(s_refs[:6]), partner_quarters(at, s_refs[6:])))
+    cots = list(zip(own_quarters(c_refs[:6]), partner_quarters(at, c_refs[6:])))
     places = places_of(at)
     length, quarter = states[0][0].shape
     grads = None
@@ -258,13 +260,14 @@
     def near(piece):
         return piece, swapped(piece, "c")
 
-    def gathered(own, relayed):
+    def gathered(own):
         up, down = moved(own, 1), moved(own, -1)
-        far = moved(up if relayed == 1 else down, relayed)
-        kinds = (own, far, up, down)
+        half = length // 2
+        low, high = moved(up[:half], 1), moved(down[half:], -1)
+        kinds = (own, low, high, up, down)
         return [part for piece in kinds for part in near(piece)]
 
-    s_parts, c_parts = gathered(states, 1), gathered(cotangent, -1)
+    s_parts, c_parts = gathered(states), gathered(cotangent)
     cos, sine = rope_tables(length, HEAD_DIM)
     width = part // 2
     wq, wk, wv, wo = kernel_call(
@@ -288,8 +291,8 @@
             (*parts, wq, wk, wv, cos, sine),
         )
 
-    partner_found = attention(True, s_parts[4:])
-    own_found = attention(False, s_parts[:4])
+    partner_found = attention(True, s_parts[6:])
+    own_found = attention(False, s_parts[:6])
     sent = kernel_call(
         blocks_body,
         shape((blocks, 2 * tall, LANES), bf16),

time: 103 us -> 105 us (1.019)
  starting transfers between devices: 23.7 us -> 26.5 us
  waiting for transfers between devices: 6.23 us -> 4.72 us
  blocking collectives: 61.9 us -> 63.1 us
    all_to_all x1, blocking collectives: 39.7 us -> 42.1 us  [on_device(): got = lax.all_to_all(sent, NEAR, 0, 0, tiled=True)]
    ppermute x6 -> x8, starting transfers between devices: 16.5 us -> 18.7 us  [moved(): return lax.ppermute(piece, ('zb', 'h'), around(step))]
    ppermute x6 -> x8, waiting for transfers between devices: 6.21 us -> 4.32 us  [moved(): return lax.ppermute(piece, ('zb', 'h'), around(step))]
    all_to_all x1, blocking collectives: 22.1 us -> 20.9 us  [on_device(): lax.all_to_all(rows, EVERY, 0, 0, tiled=True)]
    ppermute x8 -> x10, starting transfers between devices: 7.21 us -> 7.76 us  [swapped(): return lax.ppermute(value, axis, SWAP)]
  transfers between devices with their start and end apart: 14 -> 18, of which waited for: 5 -> 4; matrix products, arithmetic and copies ran while one was open for 0% -> 0% of each run, Pallas kernels for 6% -> 6%
where the time goes in v3:
time: 105 us
  blocking collectives  63.1 us (60%)
  starting transfers between devices  26.5 us (25%)
  Pallas kernels  10.5 us (10%)
  waiting for transfers between devices  4.72 us (4%)
    all_to_all x1, blocking collectives, on_device(): got = lax.all_to_all(sent, NEAR, 0, 0, tiled=True)  42.1 us
    all_to_all x1, blocking collectives, on_device(): lax.all_to_all(rows, EVERY, 0, 0, tiled=True)  20.9 us
    ppermute x8, starting transfers between devices, moved(): return lax.ppermute(piece, ('zb', 'h'), around(step))  18.7 us
    pallas_call x6, Pallas kernels, kernel_call(): pl.pallas_call(with_place, out_shape=outs, in_specs=[hbm if i in far else...  10.5 us
    ppermute x10, starting transfers between devices, swapped(): return lax.ppermute(value, axis, SWAP)  7.76 us
    ppermute x8, waiting for transfers between devices, moved(): return lax.ppermute(piece, ('zb', 'h'), around(step))  4.32 us
  transfers between devices with their start and end apart: 18, of which 4 were waited for; matrix products, arithmetic and copies ran while one was open for 0% of the time, Pallas kernels for 6%

profile of v3, /device:TPU:1, one launch (start us, length us, event | category | flops | bytes accessed | tf_op | source)
XLA Modules:
  0.0 105.0 jit_solution(15307531170047353218)
XLA Ops:
  0.0 6.8 %collective-permute-start.4 = (bf16[128,512]{1,0:T(8,128)(2,1)}, bf16[128,512]{1,0:T(8,128)(2,1)S(1)}, u32[]{:S(2)}, u32[]{:S(2)}) collective-permute-start(bf16[128,512]{1,0:T(8,128)(2,1)} %bitcast.7), channel_id=1, source_target_pairs={{0,130},{128,0},{2,128},{130,2},{1,131},{129,1},{3,129},{131,3},{4... | collective-permute-start | bytes 393224 | tf_op jit(solution)/shard_map/ppermute | solution.py:258
  6.8 3.6 %collective-permute-start.13 = (bf16[128,512]{1,0:T(8,128)(2,1)}, bf16[128,512]{1,0:T(8,128)(2,1)S(1)}, u32[]{:S(2)}, u32[]{:S(2)}) collective-permute-start(bf16[128,512]{1,0:T(8,128)(2,1)} %bitcast.13), channel_id=1, source_target_pairs={{0,130},{128,0},{2,128},{130,2},{1,131},{129,1},{3,129},{131,3},{4... | collective-permute-start | bytes 393224 | tf_op jit(solution)/shard_map/ppermute | solution.py:258
  10.4 1.5 %collective-permute-start = (bf16[128,512]{1,0:T(8,128)(2,1)}, bf16[128,512]{1,0:T(8,128)(2,1)S(1)}, u32[]{:S(2)}, u32[]{:S(2)}) collective-permute-start(bf16[128,512]{1,0:T(8,128)(2,1)} %bitcast.9), channel_id=1, source_target_pairs={{0,1},{1,0},{2,3},{3,2},{4,5},{5,4},{6,7},{7,6},{8,9},{9,8},{10,11... | collective-permute-start | bytes 393224 | tf_op jit(solution)/shard_map/ppermute | solution.py:28
  11.9 3.9 %collective-permute-start.5 = (bf16[64,512]{1,0:T(8,128)(2,1)S(1)}, bf16[64,512]{1,0:T(8,128)(2,1)S(1)}, u32[]{:S(2)}, u32[]{:S(2)}) collective-permute-start(bf16[64,512]{1,0:T(8,128)(2,1)S(1)} %slice.17), channel_id=1, source_target_pairs={{0,130},{128,0},{2,128},{130,2},{1,131},{129,1},{3,129},{131,3},{4... | collective-permute-start | bytes 196616 | tf_op jit(solution)/shard_map/ppermute | solution.py:258
  16.0 2.6 %collective-permute-start.8 = (bf16[128,512]{1,0:T(8,128)(2,1)S(1)}, bf16[128,512]{1,0:T(8,128)(2,1)S(1)}, u32[]{:S(2)}, u32[]{:S(2)}) collective-permute-start(bf16[128,512]{1,0:T(8,128)(2,1)S(1)} %collective-permute-done.4.refs_2_.refs_8_), channel_id=1, source_target_pairs={{0,1},{1,0},{2,3},{3,2},{4,5},{5,4},{6,7},{7,6},{8,9},{9,8},{10,11... | collective-permute-start | bytes 393224 | tf_op jit(solution)/shard_map/ppermute | solution.py:28
  18.6 0.2 collective-permute-done.10.refs_16_
  18.8 4.2 %collective-permute-start.14 = (bf16[64,512]{1,0:T(8,128)(2,1)S(1)}, bf16[64,512]{1,0:T(8,128)(2,1)S(1)}, u32[]{:S(2)}, u32[]{:S(2)}) collective-permute-start(bf16[64,512]{1,0:T(8,128)(2,1)S(1)} %slice.19), channel_id=1, source_target_pairs={{0,130},{128,0},{2,128},{130,2},{1,131},{129,1},{3,129},{131,3},{4... | collective-permute-start | bytes 196616 | tf_op jit(solution)/shard_map/ppermute | solution.py:258
  23.2 0.4 collective-permute-start.6
  23.5 1.2 %collective-permute-done.2.refs_2_ = bf16[64,512]{1,0:T(8,128)(2,1)S(1)} collective-permute-done((bf16[64,512]{1,0:T(8,128)(2,1)S(1)}, bf16[64,512]{1,0:T(8,128)(2,1)S(1)}, u32[]{:S(2)}, u32[]{:S(2)}) %collective-permute-start.2) | collective-permute-done | bytes 65568 | tf_op jit(solution)/shard_map/ppermute | solution.py:258
  24.8 0.6 collective-permute-start.7
  25.4 0.2 collective-permute-start.9
  25.6 2.8 %collective-permute-done.11.refs_12_ = bf16[64,512]{1,0:T(8,128)(2,1)S(1)} collective-permute-done((bf16[64,512]{1,0:T(8,128)(2,1)S(1)}, bf16[64,512]{1,0:T(8,128)(2,1)S(1)}, u32[]{:S(2)}, u32[]{:S(2)}) %collective-permute-start.11) | collective-permute-done | bytes 65568 | tf_op jit(solution)/shard_map/ppermute | solution.py:258
  28.4 1.5 %collective-permute-start.3 = (bf16[64,512]{1,0:T(8,128)(2,1)S(1)}, bf16[64,512]{1,0:T(8,128)(2,1)S(1)}, u32[]{:S(2)}, u32[]{:S(2)}) collective-permute-start(bf16[64,512]{1,0:T(8,128)(2,1)S(1)} %collective-permute-done.2.refs_2_), channel_id=1, source_target_pairs={{0,1},{1,0},{2,3},{3,2},{4,5},{5,4},{6,7},{7,6},{8,9},{9,8},{10,11... | collective-permute-start | bytes 196616 | tf_op jit(solution)/shard_map/ppermute | solution.py:28
  29.9 0.5 collective-permute-start.16
  30.4 0.4 collective-permute-done.3.refs_3_
  30.8 0.4 collective-permute-start.15
  31.3 1.9 %shard_map.82 = (bf16[2048,256]{1,0:T(8,128)(2,1)S(1)}, bf16[2048,128]{1,0:T(8,128)(2,1)S(1)}, bf16[2048,128]{1,0:T(8,128)(2,1)S(1)}, bf16[256,2048]{1,0:T(8,128)(2,1)S(1)}) custom-call(bf16[2048,512]{1,0:T(8,128)(2,1)} %refs_0_.1, bf16[2048,128]{1,0:T(8,128)(2,1)} %refs_1_.1, bf16[2048,128]{1,0:T(8,128)(2,1)} %refs_2_.1, bf16[512,2048]{1,0:T(8,128)(2,1)} %refs_3_.1), custom_call_target="tpu_custom_call" | custom-call | tf_op jit(solution)/shard_map/pallas_call | solution.py:55
  33.2 2.1 %shard_map.84 = (bf16[128,256]{1,0:T(8,128)(2,1)S(1)}, bf16[512,128]{1,0:T(8,128)(2,1)S(1)}) custom-call(bf16[128,512]{1,0:T(8,128)(2,1)S(1)} %collective-permute-done.1.refs_0_.refs_6_, bf16[128,512]{1,0:T(8,128)(2,1)S(1)} %collective-permute-done.7.refs_1_.refs_7_, bf16[128,512]{1,0:T(8,128)(2,1)S(1)} %collective-permute-done.4.refs_2_.refs_8_, ...), custom_call_target="tpu_custom_call" | custom-call | tf_op jit(solution)/shard_map/pallas_call | solution.py:55
  35.4 2.1 %shard_map.83 = (bf16[128,256]{1,0:T(8,128)(2,1)S(1)}, bf16[512,128]{1,0:T(8,128)(2,1)S(1)}) custom-call(bf16[128,512]{1,0:T(8,128)(2,1)S(1)} %bitcast.10, bf16[128,512]{1,0:T(8,128)(2,1)S(1)} %collective-permute-done.refs_1_, bf16[64,512]{1,0:T(8,128)(2,1)S(1)} %collective-permute-done.2.refs_2_, bf16[64,512]{1,0:T(8,128)(2,1)S(1)} %collective-permute-done.3.refs_3_, ...), custom_call_target="tpu_custom_call" | custom-call | tf_op jit(solution)/shard_map/pallas_call | solution.py:55
  37.6 2.2 %shard_map.85 = bf16[32,320,128]{2,1,0:T(8,128)(2,1)S(1)} custom-call(bf16[128,512]{1,0:T(8,128)(2,1)S(1)} %bitcast.11, bf16[128,512]{1,0:T(8,128)(2,1)S(1)} %collective-permute-done.refs_1_, bf16[64,512]{1,0:T(8,128)(2,1)S(1)} %collective-permute-done.2.refs_2_, bf16[64,512]{1,0:T(8,128)(2,1)S(1)} %collective-permute-done.3.refs_3_, ...), custom_call_target="tpu_custom_call" | custom-call | tf_op jit(solution)/shard_map/pallas_call | solution.py:55
  39.7 42.1 %all_to_all.10.refs_0_ = bf16[32,320,128]{2,1,0:T(8,128)(2,1)S(1)} all-to-all(bf16[32,320,128]{2,1,0:T(8,128)(2,1)S(1)} %shard_map.85), channel_id=1, replica_groups=mesh['zb'=2,'za'=2,'x'=4,'y'=4,'h'=2,'c'=2] {'za','x','y'}, dimensions={0} | all-to-all | bytes 5242880 | tf_op jit(solution)/shard_map/all_to_all | solution.py:301
  81.9 1.5 %shard_map.86 = f32[256,128]{1,0:T(8,128)S(1)} custom-call(bf16[32,320,128]{2,1,0:T(8,128)(2,1)S(1)} %all_to_all.10.refs_0_), custom_call_target="tpu_custom_call" | custom-call | tf_op jit(solution)/shard_map/pallas_call | solution.py:55
  83.4 20.9 %all_to_all.11 = f32[256,1,128]{2,1,0:T(1,128)S(1)} all-to-all(f32[256,1,128]{2,1,0:T(1,128)S(1)} %bitcast.12), channel_id=1, replica_groups=mesh['zb'=2,'za'=2,'x'=4,'y'=4,'h'=2,'c'=2] {'zb','za','x','y','h','c'}, dimensions={0} | all-to-all | bytes 262144 | tf_op jit(solution)/shard_map/all_to_all | solution.py:310
  104.3 0.6 shard_map.87
  (32 shorter events, 0.4 us)
Async XLA Ops:
  0.0 11.9 %collective-permute-start.4 = (bf16[128,512]{1,0:T(8,128)(2,1)}, bf16[128,512]{1,0:T(8,128)(2,1)S(1)}, u32[]{:S(2)}, u32[]{:S(2)}) collective-permute-start(bf16[128,512]{1,0:T(8,128)(2,1)} %bitcast.7), channel_id=1, source_target_pairs={{0,130},{128,0},{2,128},{130,2},{1,131},{129,1},{3,129},{131,3},{4... | collective-permute-start | bytes 393224 | tf_op jit(solution)/shard_map/ppermute | solution.py:258
  6.8 9.0 %collective-permute-start.1 = (bf16[128,512]{1,0:T(8,128)(2,1)}, bf16[128,512]{1,0:T(8,128)(2,1)S(1)}, u32[]{:S(2)}, u32[]{:S(2)}) collective-permute-start(bf16[128,512]{1,0:T(8,128)(2,1)} %bitcast.8), channel_id=1, source_target_pairs={{0,128},{128,2},{2,130},{130,0},{1,129},{129,3},{3,131},{131,1},{4... | collective-permute-start | bytes 393224 | tf_op jit(solution)/shard_map/ppermute | solution.py:258
  6.8 9.1 %collective-permute-start.13 = (bf16[128,512]{1,0:T(8,128)(2,1)}, bf16[128,512]{1,0:T(8,128)(2,1)S(1)}, u32[]{:S(2)}, u32[]{:S(2)}) collective-permute-start(bf16[128,512]{1,0:T(8,128)(2,1)} %bitcast.13), channel_id=1, source_target_pairs={{0,130},{128,0},{2,128},{130,2},{1,131},{129,1},{3,129},{131,3},{4... | collective-permute-start | bytes 393224 | tf_op jit(solution)/shard_map/ppermute | solution.py:258
  10.4 8.4 %collective-permute-start.10 = (bf16[128,512]{1,0:T(8,128)(2,1)}, bf16[128,512]{1,0:T(8,128)(2,1)S(1)}, u32[]{:S(2)}, u32[]{:S(2)}) collective-permute-start(bf16[128,512]{1,0:T(8,128)(2,1)} %bitcast.14), channel_id=1, source_target_pairs={{0,128},{128,2},{2,130},{130,0},{1,129},{129,3},{3,131},{131,1},{4... | collective-permute-start | bytes 393224 | tf_op jit(solution)/shard_map/ppermute | solution.py:258
  10.4 12.6 %collective-permute-start = (bf16[128,512]{1,0:T(8,128)(2,1)}, bf16[128,512]{1,0:T(8,128)(2,1)S(1)}, u32[]{:S(2)}, u32[]{:S(2)}) collective-permute-start(bf16[128,512]{1,0:T(8,128)(2,1)} %bitcast.9), channel_id=1, source_target_pairs={{0,1},{1,0},{2,3},{3,2},{4,5},{5,4},{6,7},{7,6},{8,9},{9,8},{10,11... | collective-permute-start | bytes 393224 | tf_op jit(solution)/shard_map/ppermute | solution.py:28
  11.9 11.2 %collective-permute-start.5 = (bf16[64,512]{1,0:T(8,128)(2,1)S(1)}, bf16[64,512]{1,0:T(8,128)(2,1)S(1)}, u32[]{:S(2)}, u32[]{:S(2)}) collective-permute-start(bf16[64,512]{1,0:T(8,128)(2,1)S(1)} %slice.17), channel_id=1, source_target_pairs={{0,130},{128,0},{2,128},{130,2},{1,131},{129,1},{3,129},{131,3},{4... | collective-permute-start | bytes 196616 | tf_op jit(solution)/shard_map/ppermute | solution.py:258
  15.9 8.9 %collective-permute-start.2 = (bf16[64,512]{1,0:T(8,128)(2,1)S(1)}, bf16[64,512]{1,0:T(8,128)(2,1)S(1)}, u32[]{:S(2)}, u32[]{:S(2)}) collective-permute-start(bf16[64,512]{1,0:T(8,128)(2,1)S(1)} %slice.16), channel_id=1, source_target_pairs={{0,128},{128,2},{2,130},{130,0},{1,129},{129,3},{3,131},{131,1},{4... | collective-permute-start | bytes 196616 | tf_op jit(solution)/shard_map/ppermute | solution.py:258
  16.0 13.9 %collective-permute-start.8 = (bf16[128,512]{1,0:T(8,128)(2,1)S(1)}, bf16[128,512]{1,0:T(8,128)(2,1)S(1)}, u32[]{:S(2)}, u32[]{:S(2)}) collective-permute-start(bf16[128,512]{1,0:T(8,128)(2,1)S(1)} %collective-permute-done.4.refs_2_.refs_8_), channel_id=1, source_target_pairs={{0,1},{1,0},{2,3},{3,2},{4,5},{5,4},{6,7},{7,6},{8,9},{9,8},{10,11... | collective-permute-start | bytes 393224 | tf_op jit(solution)/shard_map/ppermute | solution.py:28
  18.8 6.6 %collective-permute-start.14 = (bf16[64,512]{1,0:T(8,128)(2,1)S(1)}, bf16[64,512]{1,0:T(8,128)(2,1)S(1)}, u32[]{:S(2)}, u32[]{:S(2)}) collective-permute-start(bf16[64,512]{1,0:T(8,128)(2,1)S(1)} %slice.19), channel_id=1, source_target_pairs={{0,130},{128,0},{2,128},{130,2},{1,131},{129,1},{3,129},{131,3},{4... | collective-permute-start | bytes 196616 | tf_op jit(solution)/shard_map/ppermute | solution.py:258
  23.0 10.2 %copy-start.1 = (f32[128,128]{1,0:T(8,128)S(1)}, f32[128,128]{1,0:T(8,128)}, u32[]{:S(2)}) copy-start(f32[128,128]{1,0:T(8,128)} %constant.5.clone.refs_10_.refs_8_) | copy-start | bytes 196612
  23.0 10.2 %copy-start.2 = (f32[128,128]{1,0:T(8,128)S(1)}, f32[128,128]{1,0:T(8,128)}, u32[]{:S(2)}) copy-start(f32[128,128]{1,0:T(8,128)} %constant.4.clone.refs_9_.refs_7_) | copy-start | bytes 196612
  23.1 5.3 %collective-permute-start.11 = (bf16[64,512]{1,0:T(8,128)(2,1)S(1)}, bf16[64,512]{1,0:T(8,128)(2,1)S(1)}, u32[]{:S(2)}, u32[]{:S(2)}) collective-permute-start(bf16[64,512]{1,0:T(8,128)(2,1)S(1)} %slice.18), channel_id=1, source_target_pairs={{0,128},{128,2},{2,130},{130,0},{1,129},{129,3},{3,131},{131,1},{4... | collective-permute-start | bytes 196616 | tf_op jit(solution)/shard_map/ppermute | solution.py:258
  23.2 6.7 %collective-permute-start.6 = (bf16[64,512]{1,0:T(8,128)(2,1)S(1)}, bf16[64,512]{1,0:T(8,128)(2,1)S(1)}, u32[]{:S(2)}, u32[]{:S(2)}) collective-permute-start(bf16[64,512]{1,0:T(8,128)(2,1)S(1)} %collective-permute-done.5.refs_4_), channel_id=1, source_target_pairs={{0,1},{1,0},{2,3},{3,2},{4,5},{5,4},{6,7},{7,6},{8,9},{9,8},{10,11... | collective-permute-start | bytes 196616 | tf_op jit(solution)/shard_map/ppermute | solution.py:28
  24.8 6.3 %collective-permute-start.7 = (bf16[128,512]{1,0:T(8,128)(2,1)S(1)}, bf16[128,512]{1,0:T(8,128)(2,1)S(1)}, u32[]{:S(2)}, u32[]{:S(2)}) collective-permute-start(bf16[128,512]{1,0:T(8,128)(2,1)S(1)} %collective-permute-done.1.refs_0_.refs_6_), channel_id=1, source_target_pairs={{0,1},{1,0},{2,3},{3,2},{4,5},{5,4},{6,7},{7,6},{8,9},{9,8},{10,11... | collective-permute-start | bytes 393224 | tf_op jit(solution)/shard_map/ppermute | solution.py:28
  25.4 12.1 %collective-permute-start.9 = (bf16[128,512]{1,0:T(8,128)(2,1)}, bf16[128,512]{1,0:T(8,128)(2,1)S(1)}, u32[]{:S(2)}, u32[]{:S(2)}) collective-permute-start(bf16[128,512]{1,0:T(8,128)(2,1)} %bitcast.15), channel_id=1, source_target_pairs={{0,1},{1,0},{2,3},{3,2},{4,5},{5,4},{6,7},{7,6},{8,9},{9,8},{10,11... | collective-permute-start | bytes 393224 | tf_op jit(solution)/shard_map/ppermute | solution.py:28
  28.4 2.4 %collective-permute-start.3 = (bf16[64,512]{1,0:T(8,128)(2,1)S(1)}, bf16[64,512]{1,0:T(8,128)(2,1)S(1)}, u32[]{:S(2)}, u32[]{:S(2)}) collective-permute-start(bf16[64,512]{1,0:T(8,128)(2,1)S(1)} %collective-permute-done.2.refs_2_), channel_id=1, source_target_pairs={{0,1},{1,0},{2,3},{3,2},{4,5},{5,4},{6,7},{7,6},{8,9},{9,8},{10,11... | collective-permute-start | bytes 196616 | tf_op jit(solution)/shard_map/ppermute | solution.py:28
  29.9 7.6 %collective-permute-start.17 = (bf16[128,512]{1,0:T(8,128)(2,1)S(1)}, bf16[128,512]{1,0:T(8,128)(2,1)S(1)}, u32[]{:S(2)}, u32[]{:S(2)}) collective-permute-start(bf16[128,512]{1,0:T(8,128)(2,1)S(1)} %collective-permute-done.13.refs_18_), channel_id=1, source_target_pairs={{0,1},{1,0},{2,3},{3,2},{4,5},{5,4},{6,7},{7,6},{8,9},{9,8},{10,11... | collective-permute-start | bytes 393224 | tf_op jit(solution)/shard_map/ppermute | solution.py:28
  29.9 7.6 %collective-permute-start.16 = (bf16[128,512]{1,0:T(8,128)(2,1)S(1)}, bf16[128,512]{1,0:T(8,128)(2,1)S(1)}, u32[]{:S(2)}, u32[]{:S(2)}) collective-permute-start(bf16[128,512]{1,0:T(8,128)(2,1)S(1)} %collective-permute-done.10.refs_16_), channel_id=1, source_target_pairs={{0,1},{1,0},{2,3},{3,2},{4,5},{5,4},{6,7},{7,6},{8,9},{9,8},{10,11... | collective-permute-start | bytes 393224 | tf_op jit(solution)/shard_map/ppermute | solution.py:28
  30.8 6.7 %collective-permute-start.15 = (bf16[64,512]{1,0:T(8,128)(2,1)S(1)}, bf16[64,512]{1,0:T(8,128)(2,1)S(1)}, u32[]{:S(2)}, u32[]{:S(2)}) collective-permute-start(bf16[64,512]{1,0:T(8,128)(2,1)S(1)} %collective-permute-done.14.refs_14_), channel_id=1, source_target_pairs={{0,1},{1,0},{2,3},{3,2},{4,5},{5,4},{6,7},{7,6},{8,9},{9,8},{10,11... | collective-permute-start | bytes 196616 | tf_op jit(solution)/shard_map/ppermute | solution.py:28
  31.1 6.4 %collective-permute-start.12 = (bf16[64,512]{1,0:T(8,128)(2,1)S(1)}, bf16[64,512]{1,0:T(8,128)(2,1)S(1)}, u32[]{:S(2)}, u32[]{:S(2)}) collective-permute-start(bf16[64,512]{1,0:T(8,128)(2,1)S(1)} %collective-permute-done.11.refs_12_), channel_id=1, source_target_pairs={{0,1},{1,0},{2,3},{3,2},{4,5},{5,4},{6,7},{7,6},{8,9},{9,8},{10,11... | collective-permute-start | bytes 196616 | tf_op jit(solution)/shard_map/ppermute | solution.py:28
  33.2 2.2 %copy-start = (bf16[1,128,512]{2,1,0:T(8,128)(2,1)S(1)}, bf16[1,128,512]{2,1,0:T(8,128)(2,1)}, u32[]{:S(2)}) copy-start(bf16[1,128,512]{2,1,0:T(8,128)(2,1)} %param.8) | copy-start | bytes 393220
  33.2 4.3 %copy-start.3 = (bf16[1,128,512]{2,1,0:T(8,128)(2,1)S(1)}, bf16[1,128,512]{2,1,0:T(8,128)(2,1)}, u32[]{:S(2)}) copy-start(bf16[1,128,512]{2,1,0:T(8,128)(2,1)} %param.9) | copy-start | bytes 393220

commit v4 on v2

--- a/solution.py
+++ b/solution.py
@@ -92,21 +92,6 @@
     up, down = values[:2], values[2:]
     here = [jnp.where(straight, d, u) for u, d in zip(up, down)]
     return here + [jnp.where(straight, u, d) for u, d in zip(up, down)]
-
-
-def fetch_body(at, wq, wk, wv, wo, wq_out, wk_out, wv_out, wo_out, sems):
-    part = wq_out.shape[1]
-    half = rows_at(at[2], part)
-    moves = [
-        pltpu.make_async_copy(src, dst, sems.at[i])
-        for i, (src, dst) in enumerate(
-            ((wq.at[:, half], wq_out), (wk, wk_out), (wv, wv_out), (wo.at[half, :], wo_out))
-        )
-    ]
-    for move in moves:
-        move.start()
-    for move in moves:
-        move.wait()
 
 
 def attention_body(partner, at, *refs):
@@ -155,6 +140,24 @@
             found.append(dot(p, values))
         tile = jnp.where(low, found[0], found[1])
         attended[:, t * LANES : (t + 1) * LANES] = tile.astype(jnp.bfloat16)
+
+
+def first_attention_body(
+    at, u0, u1, d0, d1, wq, wk, wv, cos, sine, wo,
+    attended, probs, wq_out, wk_out, wv_out, cos_out, sine_out, wo_out, sems,
+):
+    half = rows_at(at[2], wq_out.shape[1])
+    sources = (wq.at[:, half], wk, wv, cos, sine, wo.at[half, :])
+    pairs = zip(sources, (wq_out, wk_out, wv_out, cos_out, sine_out, wo_out))
+    moves = [pltpu.make_async_copy(src, dst, sems.at[i]) for i, (src, dst) in enumerate(pairs)]
+    for move in moves:
+        move.start()
+    for move in moves[:5]:
+        move.wait()
+    attention_body(
+        True, at, u0, u1, d0, d1, wq_out, wk_out, wv_out, cos_out, sine_out, attended, probs
+    )
+    moves[5].wait()
 
 
 def blocks_body(at, *refs):
@@ -267,29 +270,25 @@
     s_parts, c_parts = gathered(states, 1), gathered(cotangent, -1)
     cos, sine = rope_tables(length, HEAD_DIM)
     width = part // 2
-    wq, wk, wv, wo = kernel_call(
-        fetch_body,
-        tuple(
-            shape(dims, bf16)
-            for dims in ((wq.shape[0], width), wk.shape, wv.shape, (width, wo.shape[1]))
+    found = (shape((length, width), bf16), shape((width // HEAD_DIM * length, length), bf16))
+    weights = ((wq.shape[0], width), wk.shape, wv.shape, (width, wo.shape[1]))
+    *partner_found, wq, wk, wv, cos, sine, wo = kernel_call(
+        first_attention_body,
+        (
+            *found,
+            *(shape(dims, bf16) for dims in weights[:3]),
+            *(shape(a.shape, f32) for a in (cos, sine)),
+            shape(weights[3], bf16),
         ),
-        (wq, wk, wv, wo),
-        (pltpu.SemaphoreType.DMA((4,)),),
-        far=(0, 1, 2, 3),
-    )
-
-    def attention(partner, parts):
-        return kernel_call(
-            functools.partial(attention_body, partner),
-            (
-                shape((length, width), bf16),
-                shape((width // HEAD_DIM * length, length), bf16),
-            ),
-            (*parts, wq, wk, wv, cos, sine),
-        )
-
-    partner_found = attention(True, s_parts[4:])
-    own_found = attention(False, s_parts[:4])
+        (*s_parts[4:], wq, wk, wv, jnp.asarray(cos), jnp.asarray(sine), wo),
+        (pltpu.SemaphoreType.DMA((6,)),),
+        far=(4, 5, 6, 7, 8, 9),
+    )
+    own_found = kernel_call(
+        functools.partial(attention_body, False),
+        found,
+        (*s_parts[:4], wq, wk, wv, cos, sine),
+    )
     sent = kernel_call(
         blocks_body,
         shape((blocks, 2 * tall, LANES), bf16),

time: 103 us -> 103 us (level)
  waiting for transfers between devices: 6.23 us -> 0.99 us
  starting transfers between devices: 23.7 us -> 28.9 us
    ppermute x6, waiting for transfers between devices: 6.21 us -> 0.97 us  [moved(): return lax.ppermute(piece, ('zb', 'h'), around(step))]
    ppermute x8, starting transfers between devices: 7.21 us -> 9.9 us  [swapped(): return lax.ppermute(value, axis, SWAP)]
    ppermute x6, starting transfers between devices: 16.5 us -> 19 us  [moved(): return lax.ppermute(piece, ('zb', 'h'), around(step))]
    pallas_call x6 -> x5, Pallas kernels: 10.5 us -> 10.1 us  [kernel_call(): pl.pallas_call(with_place, out_shape=outs, in_specs=[hbm if i in far else...]
  transfers between devices with their start and end apart: 14 -> 14, of which waited for: 5 -> 2; matrix products, arithmetic and copies ran while one was open for 0% -> 0% of each run, Pallas kernels for 6% -> 6%
where the time goes in v4:
time: 103 us
  blocking collectives  62.8 us (61%)
  starting transfers between devices  28.9 us (28%)
  Pallas kernels  10.1 us (10%)
    all_to_all x1, blocking collectives, on_device(): got = lax.all_to_all(sent, NEAR, 0, 0, tiled=True)  39.7 us
    all_to_all x1, blocking collectives, on_device(): lax.all_to_all(rows, EVERY, 0, 0, tiled=True)  23 us
    ppermute x6, starting transfers between devices, moved(): return lax.ppermute(piece, ('zb', 'h'), around(step))  19 us
    pallas_call x5, Pallas kernels, kernel_call(): pl.pallas_call(with_place, out_shape=outs, in_specs=[hbm if i in far else...  10.1 us
    ppermute x8, starting transfers between devices, swapped(): return lax.ppermute(value, axis, SWAP)  9.9 us
  transfers between devices with their start and end apart: 14, of which 2 were waited for; matrix products, arithmetic and copies ran while one was open for 0% of the time, Pallas kernels for 6%

profile of v4, /device:TPU:1, one launch (start us, length us, event | category | flops | bytes accessed | tf_op | source)
XLA Modules:
  0.0 102.9 jit_solution(7141892790736956704)
XLA Ops:
  0.0 3.8 %collective-permute-start.1 = (bf16[128,512]{1,0:T(8,128)(2,1)}, bf16[128,512]{1,0:T(8,128)(2,1)S(1)}, u32[]{:S(2)}, u32[]{:S(2)}) collective-permute-start(bf16[128,512]{1,0:T(8,128)(2,1)} %bitcast.7), channel_id=1, source_target_pairs={{0,128},{128,2},{2,130},{130,0},{1,129},{129,3},{3,131},{131,1},{4... | collective-permute-start | bytes 393224 | tf_op jit(solution)/shard_map/ppermute | solution.py:259
  3.8 3.0 %collective-permute-start.5 = (bf16[128,512]{1,0:T(8,128)(2,1)}, bf16[128,512]{1,0:T(8,128)(2,1)S(1)}, u32[]{:S(2)}, u32[]{:S(2)}) collective-permute-start(bf16[128,512]{1,0:T(8,128)(2,1)} %bitcast.8), channel_id=1, source_target_pairs={{0,130},{128,0},{2,128},{130,2},{1,131},{129,1},{3,129},{131,3},{4... | collective-permute-start | bytes 393224 | tf_op jit(solution)/shard_map/ppermute | solution.py:259
  6.8 1.0 collective-permute-start
  7.8 2.6 %collective-permute-start.8 = (bf16[128,512]{1,0:T(8,128)(2,1)}, bf16[128,512]{1,0:T(8,128)(2,1)S(1)}, u32[]{:S(2)}, u32[]{:S(2)}) collective-permute-start(bf16[128,512]{1,0:T(8,128)(2,1)} %bitcast.13), channel_id=1, source_target_pairs={{0,130},{128,0},{2,128},{130,2},{1,131},{129,1},{3,129},{131,3},{4... | collective-permute-start | bytes 393224 | tf_op jit(solution)/shard_map/ppermute | solution.py:259
  10.4 0.4 collective-permute-done.1.refs_0_.refs_4_
  10.8 3.0 %collective-permute-start.2 = (bf16[128,512]{1,0:T(8,128)(2,1)S(1)}, bf16[128,512]{1,0:T(8,128)(2,1)S(1)}, u32[]{:S(2)}, u32[]{:S(2)}) collective-permute-start(bf16[128,512]{1,0:T(8,128)(2,1)S(1)} %collective-permute-done.1.refs_0_.refs_4_), channel_id=1, source_target_pairs={{0,128},{128,2},{2,130},{130,0},{1,129},{129,3},{3,131},{131,1},{4... | collective-permute-start | bytes 393224 | tf_op jit(solution)/shard_map/ppermute | solution.py:259
  13.8 4.2 %collective-permute-start.11 = (bf16[128,512]{1,0:T(8,128)(2,1)}, bf16[128,512]{1,0:T(8,128)(2,1)S(1)}, u32[]{:S(2)}, u32[]{:S(2)}) collective-permute-start(bf16[128,512]{1,0:T(8,128)(2,1)} %bitcast.14), channel_id=1, source_target_pairs={{0,128},{128,2},{2,130},{130,0},{1,129},{129,3},{3,131},{131,1},{4... | collective-permute-start | bytes 393224 | tf_op jit(solution)/shard_map/ppermute | solution.py:259
  18.0 1.5 %collective-permute-start.6 = (bf16[128,512]{1,0:T(8,128)(2,1)S(1)}, bf16[128,512]{1,0:T(8,128)(2,1)S(1)}, u32[]{:S(2)}, u32[]{:S(2)}) collective-permute-start(bf16[128,512]{1,0:T(8,128)(2,1)S(1)} %collective-permute-done.5.refs_2_.refs_6_), channel_id=1, source_target_pairs={{0,1},{1,0},{2,3},{3,2},{4,5},{5,4},{6,7},{7,6},{8,9},{9,8},{10,11... | collective-permute-start | bytes 393224 | tf_op jit(solution)/shard_map/ppermute | solution.py:28
  19.5 0.1 collective-permute-start.4
  19.6 0.6 collective-permute-done.8.refs_14_
  20.2 2.4 %collective-permute-start.9 = (bf16[128,512]{1,0:T(8,128)(2,1)S(1)}, bf16[128,512]{1,0:T(8,128)(2,1)S(1)}, u32[]{:S(2)}, u32[]{:S(2)}) collective-permute-start(bf16[128,512]{1,0:T(8,128)(2,1)S(1)} %collective-permute-done.8.refs_14_), channel_id=1, source_target_pairs={{0,130},{128,0},{2,128},{130,2},{1,131},{129,1},{3,129},{131,3},{4... | collective-permute-start | bytes 393224 | tf_op jit(solution)/shard_map/ppermute | solution.py:259
  22.5 4.2 %collective-permute-start.3 = (bf16[128,512]{1,0:T(8,128)(2,1)S(1)}, bf16[128,512]{1,0:T(8,128)(2,1)S(1)}, u32[]{:S(2)}, u32[]{:S(2)}) collective-permute-start(bf16[128,512]{1,0:T(8,128)(2,1)S(1)} %collective-permute-done.2.refs_2_), channel_id=1, source_target_pairs={{0,1},{1,0},{2,3},{3,2},{4,5},{5,4},{6,7},{7,6},{8,9},{9,8},{10,11... | collective-permute-start | bytes 393224 | tf_op jit(solution)/shard_map/ppermute | solution.py:28
  26.8 1.6 %collective-permute-start.7 = (bf16[128,512]{1,0:T(8,128)(2,1)}, bf16[128,512]{1,0:T(8,128)(2,1)S(1)}, u32[]{:S(2)}, u32[]{:S(2)}) collective-permute-start(bf16[128,512]{1,0:T(8,128)(2,1)} %bitcast.15), channel_id=1, source_target_pairs={{0,1},{1,0},{2,3},{3,2},{4,5},{5,4},{6,7},{7,6},{8,9},{9,8},{10,11... | collective-permute-start | bytes 393224 | tf_op jit(solution)/shard_map/ppermute | solution.py:28
  28.4 0.0 collective-permute-start.13
  28.4 0.5 collective-permute-start.12
  28.9 1.0 collective-permute-start.10
  29.9 3.7 %shard_map.82 = (bf16[128,256]{1,0:T(8,128)(2,1)S(1)}, bf16[512,128]{1,0:T(8,128)(2,1)S(1)}, bf16[2048,256]{1,0:T(8,128)(2,1)S(1)}, bf16[2048,128]{1,0:T(8,128)(...) custom-call(bf16[128,512]{1,0:T(8,128)(2,1)S(1)} %collective-permute, ...), custom_call_target="tpu_custom_call" | custom-call | tf_op jit(solution)/shard_map/pallas_call | solution.py:55
  33.6 0.0 copy-start.1
  33.6 2.1 %shard_map.83 = (bf16[128,256]{1,0:T(8,128)(2,1)S(1)}, bf16[512,128]{1,0:T(8,128)(2,1)S(1)}) custom-call(bf16[128,512]{1,0:T(8,128)(2,1)S(1)} %bitcast.10, bf16[128,512]{1,0:T(8,128)(2,1)S(1)} %collective-permute-done.refs_1_, bf16[128,512]{1,0:T(8,128)(2,1)S(1)} %collective-permute-done.2.refs_2_, bf16[128,512]{1,0:T(8,128)(2,1)S(1)} %collective-permute-done.3.refs_3_, ...), custom_call_target="tpu_custom_call" | custom-call | tf_op jit(solution)/shard_map/pallas_call | solution.py:55
  35.8 2.2 %shard_map.84 = bf16[32,320,128]{2,1,0:T(8,128)(2,1)S(1)} custom-call(bf16[128,512]{1,0:T(8,128)(2,1)S(1)} %bitcast.11, bf16[128,512]{1,0:T(8,128)(2,1)S(1)} %collective-permute-done.refs_1_, bf16[128,512]{1,0:T(8,128)(2,1)S(1)} %collective-permute-done.2.refs_2_, bf16[128,512]{1,0:T(8,128)(2,1)S(1)} %collective-permute-done.3.refs_3_, ...), custom_call_target="tpu_custom_call" | custom-call | tf_op jit(solution)/shard_map/pallas_call | solution.py:55
  38.0 39.7 %all_to_all.10.refs_0_ = bf16[32,320,128]{2,1,0:T(8,128)(2,1)S(1)} all-to-all(bf16[32,320,128]{2,1,0:T(8,128)(2,1)S(1)} %shard_map.84), channel_id=1, replica_groups=mesh['zb'=2,'za'=2,'x'=4,'y'=4,'h'=2,'c'=2] {'za','x','y'}, dimensions={0} | all-to-all | bytes 5242880 | tf_op jit(solution)/shard_map/all_to_all | solution.py:297
  77.7 1.5 %shard_map.85 = f32[256,128]{1,0:T(8,128)S(1)} custom-call(bf16[32,320,128]{2,1,0:T(8,128)(2,1)S(1)} %all_to_all.10.refs_0_), custom_call_target="tpu_custom_call" | custom-call | tf_op jit(solution)/shard_map/pallas_call | solution.py:55
  79.3 23.0 %all_to_all.11 = f32[256,1,128]{2,1,0:T(1,128)S(1)} all-to-all(f32[256,1,128]{2,1,0:T(1,128)S(1)} %bitcast.12), channel_id=1, replica_groups=mesh['zb'=2,'za'=2,'x'=4,'y'=4,'h'=2,'c'=2] {'zb','za','x','y','h','c'}, dimensions={0} | all-to-all | bytes 262144 | tf_op jit(solution)/shard_map/all_to_all | solution.py:306
  102.3 0.6 shard_map.86
  (15 shorter events, 0.0 us)
Async XLA Ops:
  0.0 10.8 %collective-permute-start.1 = (bf16[128,512]{1,0:T(8,128)(2,1)}, bf16[128,512]{1,0:T(8,128)(2,1)S(1)}, u32[]{:S(2)}, u32[]{:S(2)}) collective-permute-start(bf16[128,512]{1,0:T(8,128)(2,1)} %bitcast.7), channel_id=1, source_target_pairs={{0,128},{128,2},{2,130},{130,0},{1,129},{129,3},{3,131},{131,1},{4... | collective-permute-start | bytes 393224 | tf_op jit(solution)/shard_map/ppermute | solution.py:259
  3.8 14.2 %collective-permute-start.5 = (bf16[128,512]{1,0:T(8,128)(2,1)}, bf16[128,512]{1,0:T(8,128)(2,1)S(1)}, u32[]{:S(2)}, u32[]{:S(2)}) collective-permute-start(bf16[128,512]{1,0:T(8,128)(2,1)} %bitcast.8), channel_id=1, source_target_pairs={{0,130},{128,0},{2,128},{130,2},{1,131},{129,1},{3,129},{131,3},{4... | collective-permute-start | bytes 393224 | tf_op jit(solution)/shard_map/ppermute | solution.py:259
  6.8 12.7 %collective-permute-start = (bf16[128,512]{1,0:T(8,128)(2,1)}, bf16[128,512]{1,0:T(8,128)(2,1)S(1)}, u32[]{:S(2)}, u32[]{:S(2)}) collective-permute-start(bf16[128,512]{1,0:T(8,128)(2,1)} %bitcast.9), channel_id=1, source_target_pairs={{0,1},{1,0},{2,3},{3,2},{4,5},{5,4},{6,7},{7,6},{8,9},{9,8},{10,11... | collective-permute-start | bytes 393224 | tf_op jit(solution)/shard_map/ppermute | solution.py:28
  7.8 25.8 %copy-start = (bf16[1,128,512]{2,1,0:T(8,128)(2,1)S(1)}, bf16[1,128,512]{2,1,0:T(8,128)(2,1)}, u32[]{:S(2)}) copy-start(bf16[1,128,512]{2,1,0:T(8,128)(2,1)} %param.8) | copy-start | bytes 393220
  7.8 12.4 %collective-permute-start.8 = (bf16[128,512]{1,0:T(8,128)(2,1)}, bf16[128,512]{1,0:T(8,128)(2,1)S(1)}, u32[]{:S(2)}, u32[]{:S(2)}) collective-permute-start(bf16[128,512]{1,0:T(8,128)(2,1)} %bitcast.13), channel_id=1, source_target_pairs={{0,130},{128,0},{2,128},{130,2},{1,131},{129,1},{3,129},{131,3},{4... | collective-permute-start | bytes 393224 | tf_op jit(solution)/shard_map/ppermute | solution.py:259
  10.8 11.7 %collective-permute-start.2 = (bf16[128,512]{1,0:T(8,128)(2,1)S(1)}, bf16[128,512]{1,0:T(8,128)(2,1)S(1)}, u32[]{:S(2)}, u32[]{:S(2)}) collective-permute-start(bf16[128,512]{1,0:T(8,128)(2,1)S(1)} %collective-permute-done.1.refs_0_.refs_4_), channel_id=1, source_target_pairs={{0,128},{128,2},{2,130},{130,0},{1,129},{129,3},{3,131},{131,1},{4... | collective-permute-start | bytes 393224 | tf_op jit(solution)/shard_map/ppermute | solution.py:259
  13.8 13.0 %collective-permute-start.11 = (bf16[128,512]{1,0:T(8,128)(2,1)}, bf16[128,512]{1,0:T(8,128)(2,1)S(1)}, u32[]{:S(2)}, u32[]{:S(2)}) collective-permute-start(bf16[128,512]{1,0:T(8,128)(2,1)} %bitcast.14), channel_id=1, source_target_pairs={{0,128},{128,2},{2,130},{130,0},{1,129},{129,3},{3,131},{131,1},{4... | collective-permute-start | bytes 393224 | tf_op jit(solution)/shard_map/ppermute | solution.py:259
  18.0 10.4 %collective-permute-start.6 = (bf16[128,512]{1,0:T(8,128)(2,1)S(1)}, bf16[128,512]{1,0:T(8,128)(2,1)S(1)}, u32[]{:S(2)}, u32[]{:S(2)}) collective-permute-start(bf16[128,512]{1,0:T(8,128)(2,1)S(1)} %collective-permute-done.5.refs_2_.refs_6_), channel_id=1, source_target_pairs={{0,1},{1,0},{2,3},{3,2},{4,5},{5,4},{6,7},{7,6},{8,9},{9,8},{10,11... | collective-permute-start | bytes 393224 | tf_op jit(solution)/shard_map/ppermute | solution.py:28
  19.5 8.9 %collective-permute-start.4 = (bf16[128,512]{1,0:T(8,128)(2,1)S(1)}, bf16[128,512]{1,0:T(8,128)(2,1)S(1)}, u32[]{:S(2)}, u32[]{:S(2)}) collective-permute-start(bf16[128,512]{1,0:T(8,128)(2,1)S(1)} %collective-permute-done.1.refs_0_.refs_4_), channel_id=1, source_target_pairs={{0,1},{1,0},{2,3},{3,2},{4,5},{5,4},{6,7},{7,6},{8,9},{9,8},{10,11... | collective-permute-start | bytes 393224 | tf_op jit(solution)/shard_map/ppermute | solution.py:28
  20.2 8.7 %collective-permute-start.9 = (bf16[128,512]{1,0:T(8,128)(2,1)S(1)}, bf16[128,512]{1,0:T(8,128)(2,1)S(1)}, u32[]{:S(2)}, u32[]{:S(2)}) collective-permute-start(bf16[128,512]{1,0:T(8,128)(2,1)S(1)} %collective-permute-done.8.refs_14_), channel_id=1, source_target_pairs={{0,130},{128,0},{2,128},{130,2},{1,131},{129,1},{3,129},{131,3},{4... | collective-permute-start | bytes 393224 | tf_op jit(solution)/shard_map/ppermute | solution.py:259
  22.5 11.1 %collective-permute-start.3 = (bf16[128,512]{1,0:T(8,128)(2,1)S(1)}, bf16[128,512]{1,0:T(8,128)(2,1)S(1)}, u32[]{:S(2)}, u32[]{:S(2)}) collective-permute-start(bf16[128,512]{1,0:T(8,128)(2,1)S(1)} %collective-permute-done.2.refs_2_), channel_id=1, source_target_pairs={{0,1},{1,0},{2,3},{3,2},{4,5},{5,4},{6,7},{7,6},{8,9},{9,8},{10,11... | collective-permute-start | bytes 393224 | tf_op jit(solution)/shard_map/ppermute | solution.py:28
  26.8 9.0 %collective-permute-start.7 = (bf16[128,512]{1,0:T(8,128)(2,1)}, bf16[128,512]{1,0:T(8,128)(2,1)S(1)}, u32[]{:S(2)}, u32[]{:S(2)}) collective-permute-start(bf16[128,512]{1,0:T(8,128)(2,1)} %bitcast.15), channel_id=1, source_target_pairs={{0,1},{1,0},{2,3},{3,2},{4,5},{5,4},{6,7},{7,6},{8,9},{9,8},{10,11... | collective-permute-start | bytes 393224 | tf_op jit(solution)/shard_map/ppermute | solution.py:28
  28.4 7.4 %collective-permute-start.13 = (bf16[128,512]{1,0:T(8,128)(2,1)S(1)}, bf16[128,512]{1,0:T(8,128)(2,1)S(1)}, u32[]{:S(2)}, u32[]{:S(2)}) collective-permute-start(bf16[128,512]{1,0:T(8,128)(2,1)S(1)} %collective-permute-done.8.refs_14_), channel_id=1, source_target_pairs={{0,1},{1,0},{2,3},{3,2},{4,5},{5,4},{6,7},{7,6},{8,9},{9,8},{10,11... | collective-permute-start | bytes 393224 | tf_op jit(solution)/shard_map/ppermute | solution.py:28
  28.4 7.4 %collective-permute-start.12 = (bf16[128,512]{1,0:T(8,128)(2,1)S(1)}, bf16[128,512]{1,0:T(8,128)(2,1)S(1)}, u32[]{:S(2)}, u32[]{:S(2)}) collective-permute-start(bf16[128,512]{1,0:T(8,128)(2,1)S(1)} %collective-permute-done.11.refs_12_), channel_id=1, source_target_pairs={{0,1},{1,0},{2,3},{3,2},{4,5},{5,4},{6,7},{7,6},{8,9},{9,8},{10,11... | collective-permute-start | bytes 393224 | tf_op jit(solution)/shard_map/ppermute | solution.py:28
  28.9 6.9 %collective-permute-start.10 = (bf16[128,512]{1,0:T(8,128)(2,1)S(1)}, bf16[128,512]{1,0:T(8,128)(2,1)S(1)}, u32[]{:S(2)}, u32[]{:S(2)}) collective-permute-start(bf16[128,512]{1,0:T(8,128)(2,1)S(1)} %collective-permute-done.9.refs_10_), channel_id=1, source_target_pairs={{0,1},{1,0},{2,3},{3,2},{4,5},{5,4},{6,7},{7,6},{8,9},{9,8},{10,11... | collective-permute-start | bytes 393224 | tf_op jit(solution)/shard_map/ppermute | solution.py:28
  33.6 2.2 %copy-start.1 = (bf16[1,128,512]{2,1,0:T(8,128)(2,1)S(1)}, bf16[1,128,512]{2,1,0:T(8,128)(2,1)}, u32[]{:S(2)}) copy-start(bf16[1,128,512]{2,1,0:T(8,128)(2,1)} %param.9) | copy-start | bytes 393220
